TPU v7x, 32 devices: a whole 2x2x4 slice. The times are simulated.
32 devices in a mesh: param: 16 (over z, y, x), sensor: 2 (over core).
Axes of the slice: x: 2, y: 2, z: 4, core: 2. Of those that a mesh axis runs over, the one named last changes fastest.
Arguments:
- data: float32 [16, 512, 420], P(None, ('sensor', 'param')), may hold values from -6 to 6
- spectra: float32 [2, 512, 64, 421], P(None, 'sensor', 'param'), may hold values from -2 to 2
Outputs:
- gradient: float32 [16, 64, 420], P(None, 'param')
- rms: float32 [16], replicated
All inputs are finite; a program needn't handle non-finite values.
Results may differ from a plain program's by a relative error of at most 0.0003.
Values sent between devices are 32-bit elements; how exact they have to be, the bound alone decides.
A program may use at most 128 MiB of HBM per device.

v0:
```python
import functools
import math

import jax
import jax.numpy as jnp
import numpy as np
from jax import lax
from jax.experimental import pallas as pl
from jax.experimental.pallas import tpu as pltpu
from jax.sharding import PartitionSpec as P

MESH = pl.DeviceIdType.MESH
LANES = 128
GROUP = 8
CHUNKS = 8


def spectral_tables(steps):
    length = 2 * steps
    freqs = steps + 1
    times = lax.broadcasted_iota(jnp.int32, (steps, freqs), 0)
    bins = lax.broadcasted_iota(jnp.int32, (steps, freqs), 1)
    phase = 2.0 * math.pi / length * (times * bins % length).astype(jnp.float32)
    forward = jnp.concatenate([jnp.cos(phase), -jnp.sin(phase)], axis=1)
    weight = jnp.where((bins == 0) | (bins == steps), 1.0, 2.0) / length
    backward = jnp.concatenate([(weight * jnp.cos(phase)).T, (-weight * jnp.sin(phase)).T], axis=0)
    return (forward, backward)


def to_spectrum(series, forward):
    vectors, sensors, steps = series.shape
    flat = jnp.dot(
        series.reshape(vectors * sensors, steps),
        forward,
        precision=lax.Precision.HIGHEST,
        preferred_element_type=jnp.float32,
    )
    return flat.reshape(vectors, sensors, forward.shape[1])


def contract(kernel, spectrum):
    return jnp.einsum(
        "spf,rsf->rpf",
        kernel,
        spectrum,
        precision=lax.Precision.HIGHEST,
        preferred_element_type=jnp.float32,
    )


def general_body(data, spectra):
    steps = data.shape[2]
    freqs = steps + 1
    forward, backward = spectral_tables(steps)
    whole = to_spectrum(lax.all_gather(data, "param", axis=1, tiled=True), forward)
    real_part = whole[..., :freqs]
    imag_part = whole[..., freqs:]
    kernel_re = spectra[0]
    kernel_im = spectra[1]
    out_re = contract(kernel_re, real_part) + contract(kernel_im, imag_part)
    out_im = contract(kernel_re, imag_part) - contract(kernel_im, real_part)
    vectors, points = (out_re.shape[0], out_re.shape[1])
    stacked = jnp.concatenate([out_re, out_im], axis=2).reshape(vectors * points, 2 * freqs)
    partial_field = jnp.dot(
        stacked, backward, precision=lax.Precision.HIGHEST, preferred_element_type=jnp.float32
    ).reshape(vectors, points, steps)
    count = points * lax.axis_size("param") * steps
    share = lax.psum_scatter(partial_field, "sensor", scatter_dimension=0, tiled=True)
    squares = lax.psum(jnp.sum(share * share, axis=(1, 2)), "param")
    scale = jnp.sqrt(squares / count + 1e-06)
    normalized = share / scale[:, None, None]
    gradient, rms_all = (
        lax.all_gather(normalized, "sensor", axis=0, tiled=True),
        lax.all_gather(scale, "sensor", axis=0, tiled=True),
    )
    return (gradient, rms_all)


def split(value):
    high = value.astype(jnp.bfloat16)
    return high, (value - high.astype(jnp.float32)).astype(jnp.bfloat16)


NT_DIMS = (((1,), (1,)), ((), ()))


def product(left, right, dims):
    dot = functools.partial(lax.dot_general, dimension_numbers=dims, preferred_element_type=jnp.float32)
    size = left[0].shape[0]
    both = dot(jnp.concatenate(left, axis=0), right[0])
    return both[:size] + (both[size:] + dot(left[0], right[1]))


def kernel(
    n, lines, vectors, local, steps, points, freqs, padded, wide,
    data_ref, spectra_ref, table_ref,
    out_ref, rms_ref,
    gathered, kbuf, table, even_h, even_l, odd_h, odd_l, spectrum, product_s, partial, pairs, square, squares,
    load_sem, swap_send, swap_recv, kswap_send, kswap_recv, z_send, z_recv, y_send, y_recv, c_send, c_recv,
    f_send, f_recv, r_send, r_recv,
):
    me = lax.axis_index("param")
    core = lax.axis_index("sensor")
    x = lax.rem(me, 2)
    y = lax.rem(me // 2, 2)
    z = me // 4
    plane = 4
    other_chip = me + 1 - 2 * x
    y_chip = me + 2 - 4 * y
    other_core = 1 - core
    swapped = x != core
    kept = x == core
    per = (vectors // 2) // CHUNKS

    table_copy = pltpu.make_async_copy(table_ref, table, load_sem.at[0])
    table_copy.start()
    kbuf[:, freqs:] = jnp.zeros((2, padded - freqs) + tuple(kbuf.shape[2:]), jnp.float32)

    barrier = pltpu.get_barrier_semaphore()

    @pl.loop(1, n)
    def _(step):
        pl.semaphore_signal(barrier, inc=1, device_id=(lax.rem(me + step, n), core), device_id_type=MESH)

    pl.semaphore_signal(barrier, inc=1, device_id=(me, other_core), device_id_type=MESH)
    pl.semaphore_signal(barrier, inc=1, device_id=(other_chip, other_core), device_id_type=MESH)
    pl.semaphore_wait(barrier, n + 1)

    def slot(line, row, column):
        return line * plane + row * 2 + column

    def block(chunk, position):
        return gathered.at[pl.ds(chunk * per, per), pl.ds(pl.multiple_of(position * local, local), local), :]

    mine = slot(z, y, core)

    def swap(chunk):
        return pltpu.make_async_remote_copy(
            src_ref=data_ref.at[pl.ds(chunk * per, per)],
            dst_ref=block(chunk, slot(z, y, other_core)),
            send_sem=swap_send.at[chunk], recv_sem=swap_recv.at[chunk],
            device_id=(other_chip, other_core), device_id_type=MESH,
        )

    def swap_arrival(chunk):
        return pltpu.make_async_remote_copy(
            src_ref=data_ref.at[pl.ds(chunk * per, per)], dst_ref=block(chunk, mine),
            send_sem=swap_send.at[chunk], recv_sem=swap_recv.at[chunk],
            device_id=(other_chip, other_core), device_id_type=MESH,
        )

    def keep(chunk):
        return pltpu.make_async_copy(data_ref.at[pl.ds(chunk * per, per)], block(chunk, mine), swap_recv.at[chunk])

    def kswap(part):
        return pltpu.make_async_remote_copy(
            src_ref=spectra_ref.at[part], dst_ref=kbuf.at[part, pl.ds(0, freqs)],
            send_sem=kswap_send.at[part], recv_sem=kswap_recv.at[part],
            device_id=(other_chip, other_core), device_id_type=MESH,
        )

    def kkeep(part):
        return pltpu.make_async_copy(spectra_ref.at[part], kbuf.at[part, pl.ds(0, freqs)], kswap_recv.at[part])

    @pl.when(swapped)
    def _():
        for chunk in range(CHUNKS):
            swap(chunk).start()
        for part in range(2):
            kswap(part).start()

    @pl.when(kept)
    def _():
        for chunk in range(CHUNKS):
            keep(chunk).start()
        for part in range(2):
            kkeep(part).start()

    def send(chunk, position, target, send_sem, recv_sem):
        return pltpu.make_async_remote_copy(
            src_ref=block(chunk, position), dst_ref=block(chunk, position),
            send_sem=send_sem, recv_sem=recv_sem, device_id=target, device_id_type=MESH,
        )

    def line_copy(chunk, step, way):
        source = jnp.clip(z - way * step, 0, lines - 1)
        target = jnp.clip(z + way, 0, lines - 1)
        index = step if way > 0 else lines + step
        return send(
            chunk, slot(source, y, core), (slot(target, y, x), core), z_send.at[chunk, index], z_recv.at[chunk, index]
        )

    def line_arrival(chunk, step, way):
        source = jnp.clip(z - way * (step + 1), 0, lines - 1)
        target = jnp.clip(z + way, 0, lines - 1)
        index = step if way > 0 else lines + step
        return source, send(
            chunk, slot(source, y, core), (slot(target, y, x), core), z_send.at[chunk, index], z_recv.at[chunk, index]
        )

    def sends(step, way):
        inside = z + 1 < lines if way > 0 else z > 0
        begun = z >= step if way > 0 else z + step < lines
        return jnp.logical_and(inside, begun)

    def receives(step, way):
        return z >= step + 1 if way > 0 else z + step + 1 < lines

    def y_copy(chunk, line):
        return send(chunk, slot(line, y, core), (y_chip, core), y_send.at[chunk, line], y_recv.at[chunk, line])

    def y_arrival(chunk, line):
        return send(chunk, slot(line, 1 - y, core), (y_chip, core), y_send.at[chunk, line], y_recv.at[chunk, line])

    def core_copy(chunk, row, line):
        index = row * lines + line
        return send(chunk, slot(line, row, core), (me, other_core), c_send.at[chunk, index], c_recv.at[chunk, index])

    def core_arrival(chunk, row, line):
        index = row * lines + line
        return send(
            chunk, slot(line, row, other_core), (me, other_core), c_send.at[chunk, index], c_recv.at[chunk, index]
        )

    def start_lines(chunk):
        @pl.when(swapped)
        def _():
            swap_arrival(chunk).wait_recv()

        @pl.when(kept)
        def _():
            keep(chunk).wait()

        for way in (1, -1):

            @pl.when(sends(0, way))
            def _():
                line_copy(chunk, 0, way).start()

        y_copy(chunk, z).start()
        core_copy(chunk, y, z).start()

    def from_lines(chunk, step):
        for way in (1, -1):

            @pl.when(receives(step, way))
            def _():
                source, arrival = line_arrival(chunk, step, way)
                arrival.wait_recv()
                if step + 1 < lines - 1:

                    @pl.when(sends(step + 1, way))
                    def _():
                        line_copy(chunk, step + 1, way).start()

                y_copy(chunk, source).start()
                core_copy(chunk, y, source).start()

    def from_row(chunk):
        for step in range(lines):
            line = lax.rem(z + step, lines)
            y_arrival(chunk, line).wait_recv()
            core_copy(chunk, 1 - y, line).start()

    def from_core(chunk):
        for line in range(lines):
            for row in range(2):
                core_arrival(chunk, row, line).wait_recv()

    def transform(chunk):
        @pl.loop(0, per)
        def _(pair):
            r2 = chunk * per + pair
            for half, high, low in ((0, even_h, even_l), (1, odd_h, odd_l)):
                begin = half * (gathered.shape[2] - wide)
                series = split(gathered[r2, :, begin : begin + wide])

                @pl.loop(0, 2)
                def _(imag):
                    rows = pl.ds(pl.multiple_of(imag * padded, 16), padded)
                    result = product((high[rows, :], low[rows, :]), series, NT_DIMS)
                    for lane in range(2):
                        spectrum[lane, pl.ds(imag * vectors + 2 * r2 + half, padded, stride=2 * vectors), :] = result[
                            :, lane * LANES : (lane + 1) * LANES
                        ]

    pl.loop(0, CHUNKS)(start_lines)

    table_copy.wait()
    shift = 2 * steps - (gathered.shape[2] - wide) - steps
    values = table[...]
    even_h[...], even_l[...] = split(values)
    odd_h[...], odd_l[...] = split(pltpu.roll(values, shift, 1))

    def finish(chunk):
        from_core(chunk)
        transform(chunk)

    stages = [functools.partial(from_lines, step=step) for step in range(lines - 1)] + [from_row, finish]

    @pl.loop(0, CHUNKS + len(stages) - 1)
    def _(turn):
        for age, stage in enumerate(stages):
            chunk = turn - age

            @pl.when(jnp.logical_and(chunk >= 0, chunk < CHUNKS))
            def _():
                stage(chunk)

    @pl.when(swapped)
    def _():
        for part in range(2):
            kswap(part).wait_recv()

    @pl.when(kept)
    def _():
        for part in range(2):
            kkeep(part).wait()

    rows = GROUP * points
    columns = GROUP * 2 * vectors
    row_freq = lax.broadcasted_iota(jnp.int32, (2 * rows, columns), 0) // points % GROUP
    col_freq = lax.broadcasted_iota(jnp.int32, (2 * rows, columns), 1) // (2 * vectors)
    own = row_freq == col_freq
    lane = lax.broadcasted_iota(jnp.int32, (rows, LANES), 1)
    sign = jnp.where(lane % (2 * vectors) < vectors, 1.0, -1.0)
    row = lax.broadcasted_iota(jnp.int32, (rows, LANES), 0) // points

    @pl.loop(0, padded // GROUP, unroll=3)
    def _(group):
        begin = pl.multiple_of(group * columns, columns)
        right = split(
            jnp.concatenate([spectrum[0, pl.ds(begin, columns), :], spectrum[1, pl.ds(begin, columns), :]], axis=1)
        )
        left = jnp.concatenate(
            [kbuf[part, pl.ds(group * GROUP, GROUP)].reshape(rows, kbuf.shape[3]) for part in range(2)], axis=0
        )
        found = jnp.where(own, product(split(left), right, NT_DIMS), 0.0)
        width = columns
        while width > LANES:
            width //= 2
            found = found[:, :width] + found[:, width:]
        hop = LANES // 2
        while hop >= 2 * vectors:
            found = found + pltpu.roll(found, hop, 1)
            hop //= 2
        value = found[:rows] + sign * pltpu.roll(found[rows:], vectors, 1)
        freq = row + group * GROUP
        weight = jnp.where((freq == 0) | (freq == freqs - 1), 0.5 / steps, 1.0 / steps)
        product_s[pl.ds(pl.multiple_of(group * rows, rows), rows), :] = value * weight

    lanes = lax.broadcasted_iota(jnp.int32, (padded, LANES), 1) // (2 * vectors)
    merged = jnp.zeros((padded, LANES), jnp.float32)
    for point in range(points):
        merged = jnp.where(lanes == point, product_s[pl.ds(point, padded, stride=points), :], merged)
    turned = split(merged.T)
    plain = (((1,), (0,)), ((), ()))
    real = product(turned, (even_h[:padded, :], even_l[:padded, :]), plain)
    imag = product(turned, (even_h[padded:, :], even_l[padded:, :]), plain)
    for point in range(points):
        first = point * 2 * vectors
        field = real[first : first + vectors] + imag[first + vectors : first + 2 * vectors]
        partial[point * vectors : (point + 1) * vectors, :] = field

    def field_copy(target):
        return pltpu.make_async_remote_copy(
            src_ref=partial, dst_ref=pairs.at[x], send_sem=f_send.at[target], recv_sem=f_recv.at[x],
            device_id=(me - x + core, target), device_id_type=MESH,
        )

    def field_arrival(group):
        return pltpu.make_async_remote_copy(
            src_ref=partial, dst_ref=pairs.at[group], send_sem=f_send.at[0], recv_sem=f_recv.at[group],
            device_id=(other_chip, other_core), device_id_type=MESH,
        )

    @pl.when(swapped)
    def _():
        field_copy(0).start()
        field_copy(1).start()

    @pl.when(kept)
    def _():
        field_copy(other_core).start()
        pairs[x] = partial[...]

    field_arrival(1 - x).wait_recv()

    @pl.when(swapped)
    def _():
        field_arrival(x).wait_recv()

    total = pairs[0] + pairs[1]
    energy = total * total
    folded = energy[:vectors]
    for point in range(1, points):
        folded = folded + energy[point * vectors : (point + 1) * vectors]
    summed = jnp.broadcast_to(jnp.sum(folded, axis=1, keepdims=True), (vectors, LANES))
    square[...] = summed
    squares[me] = summed

    def square_copy(step):
        return pltpu.make_async_remote_copy(
            src_ref=square, dst_ref=squares.at[me], send_sem=r_send.at[step], recv_sem=r_recv.at[step],
            device_id=(lax.rem(me + step, n), core), device_id_type=MESH,
        )

    def square_arrival(step):
        return pltpu.make_async_remote_copy(
            src_ref=square, dst_ref=squares.at[lax.rem(me + n - step, n)],
            send_sem=r_send.at[step], recv_sem=r_recv.at[step],
            device_id=(lax.rem(me + step, n), core), device_id_type=MESH,
        )

    @pl.loop(1, n)
    def _(step):
        square_copy(step).start()

    @pl.loop(0, CHUNKS)
    def _(chunk):
        for step in range(lines - 1):
            for way in (1, -1):

                @pl.when(sends(step, way))
                def _():
                    line_copy(chunk, step, way).wait_send()

        for line in range(lines):
            y_copy(chunk, line).wait_send()
            for row in range(2):
                core_copy(chunk, row, line).wait_send()

    @pl.when(swapped)
    def _():
        for chunk in range(CHUNKS):
            swap(chunk).wait_send()
        for part in range(2):
            kswap(part).wait_send()
        field_copy(0).wait_send()
        field_copy(1).wait_send()

    @pl.when(kept)
    def _():
        field_copy(other_core).wait_send()

    @pl.loop(1, n)
    def _(step):
        square_arrival(step).wait()

    energy_all = squares[0]
    for device in range(1, n):
        energy_all = energy_all + squares[device]
    scale = jnp.sqrt(energy_all / (points * n * steps) + 1e-06)
    rms_ref[...] = scale
    inverse = scale[:, :1]
    for point in range(points):
        out_ref[point] = total[point * vectors : (point + 1) * vectors, :steps] / inverse


def paired_body(data, spectra):
    n = lax.axis_size("param")
    vectors, local, steps = data.shape
    sensors, points, freqs = spectra.shape[1:]
    wide = -(-steps // LANES) * LANES
    packed = -(-2 * steps // LANES) * LANES
    padded = -(-freqs // 16) * 16
    times = np.arange(steps)[None, :]
    bins = np.arange(freqs)[:, None]
    phase = np.pi / steps * (times * bins % (2 * steps))
    host = np.zeros((2, padded, wide), np.float32)
    host[0, :freqs, :steps] = np.cos(phase)
    host[1, :freqs, :steps] = -np.sin(phase)
    table = jnp.asarray(host.reshape(2 * padded, wide))
    lines = n // 4

    halves = data.reshape(vectors // 2, 2, local, steps)
    series = jnp.concatenate([halves[:, 0], halves[:, 1]], axis=-1)
    series = jnp.pad(series, ((0, 0), (0, 0), (0, packed - 2 * steps)))
    turned = jnp.transpose(spectra, (0, 3, 2, 1))

    hbm = pl.BlockSpec(memory_space=pl.ANY)
    vmem = pl.BlockSpec(memory_space=pltpu.VMEM)
    dma = pltpu.SemaphoreType.DMA
    f32, bf16 = jnp.float32, jnp.bfloat16
    fields, scale = pl.pallas_call(
        functools.partial(kernel, n, lines, vectors, local, steps, points, freqs, padded, wide),
        out_shape=(
            jax.ShapeDtypeStruct((points, vectors, steps), f32),
            jax.ShapeDtypeStruct((vectors, LANES), f32),
        ),
        in_specs=[hbm, hbm, hbm],
        out_specs=(vmem, vmem),
        scratch_shapes=[
            pltpu.VMEM((vectors // 2, sensors, packed), f32),
            pltpu.VMEM((2, padded, points, sensors), f32),
            pltpu.VMEM((2 * padded, wide), f32),
            pltpu.VMEM((2 * padded, wide), bf16),
            pltpu.VMEM((2 * padded, wide), bf16),
            pltpu.VMEM((2 * padded, wide), bf16),
            pltpu.VMEM((2 * padded, wide), bf16),
            pltpu.VMEM((2, padded * 2 * vectors, LANES), f32),
            pltpu.VMEM((padded * points, LANES), f32),
            pltpu.VMEM((points * vectors, wide), f32),
            pltpu.VMEM((2, points * vectors, wide), f32),
            pltpu.VMEM((vectors, LANES), f32),
            pltpu.VMEM((n, vectors, LANES), f32),
            dma((1,)),
            dma((CHUNKS,)), dma((CHUNKS,)),
            dma((2,)), dma((2,)),
            dma((CHUNKS, 2 * lines)), dma((CHUNKS, 2 * lines)),
            dma((CHUNKS, lines)), dma((CHUNKS, lines)),
            dma((CHUNKS, 2 * lines)), dma((CHUNKS, 2 * lines)),
            dma((2,)), dma((2,)),
            dma((n,)), dma((n,)),
        ],
        compiler_params=pltpu.CompilerParams(
            collective_id=0, has_side_effects=True, vmem_limit_bytes=60 * 1024 * 1024
        ),
    )(series, turned, table)
    return (jnp.transpose(fields, (1, 0, 2)), scale[:, 0])


def solution(mesh):
    in_specs = (P(None, ("sensor", "param"), None), P(None, "sensor", "param", None))
    out_specs = (P(None, "param", None), P())
    n = mesh.shape["param"]
    pair = mesh.shape["sensor"] == 2 and n == 16

    def body(data, spectra):
        vectors, local, _ = data.shape
        sensors, points = spectra.shape[1:3]
        fits = local % 8 == 0 and sensors == 2 * LANES and vectors % (2 * CHUNKS) == 0
        fits = fits and vectors % 8 == 0 and points * 2 * vectors == LANES
        return (paired_body if pair and fits else general_body)(data, spectra)

    return jax.shard_map(body, mesh=mesh, in_specs=in_specs, out_specs=out_specs, check_vma=False)
```

profile of v0, /device:TPU:0, one launch (start us, length us, event | category | flops | bytes accessed | tf_op | source)
XLA Modules:
  0.0 94.3 jit_solution(3576791516763925318)
XLA Ops:
  0.6 1.1 %slice_bitcast_fusion.1 = (f32[8,16,420]{2,1,0:T(8,128)S(1)}, f32[8,16,420]{2,1,0:T(8,128)S(1)}) fusion(f32[8,2,16,420]{3,2,1,0:T(8,128)} %bitcast.12), kind=kLoop, calls=%fused_computation.3 | loop fusion | bytes 860160 | tf_op jit(solution)/shard_map/squeeze | solution.py:477
  1.7 0.9 select_maximum_fusion.data_ref
  2.6 88.7 %shard_map.50 = (f32[4,16,420]{2,1,0:T(8,128)}, f32[16,128]{1,0:T(8,128)}) custom-call(f32[8,16,896]{2,1,0:T(8,128)} %select_maximum_fusion.data_ref, f32[2,421,4,256]{3,2,1,0:T(4,128)} %bitcast.11, f32[864,512]{1,0:T(8,128)} %constant.5.clone.table_ref), custom_call_target="tpu_custom_call" | custom-call | tf_op jit(solution)/shard_map/pallas_call | solution.py:485
  91.3 1.6 %copy.8 = f32[16,4,420]{2,1,0:T(4,128)} copy(f32[16,4,420]{2,0,1:T(8,128)} %bitcast.13) | data formatting | bytes 215040
  92.9 1.3 %slice_reduce_fusion = f32[16]{0:T(128)} fusion(f32[16,128]{1,0:T(8,128)} %get-tuple-element.5), kind=kLoop, calls=%fused_computation.4 | loop fusion | bytes 128 | tf_op jit(solution)/shard_map/slice | solution.py:520
where the time goes:
time: 95.4 us; the launch traced here: 94.3 us
  Pallas kernels  88.7 us (93%)
  local copies, waits for them, and re-layouts  4.04 us (4%)
    pallas_call x1, Pallas kernels, paired_body(): pl.pallas_call(functools.partial(kernel, n, lines, vectors, local, steps,...  88.7 us

commit v1 on v0

v1 whole, which is shorter than its diff:
```python
import functools
import math

import jax
import jax.numpy as jnp
import numpy as np
from jax import lax
from jax.experimental import pallas as pl
from jax.experimental.pallas import tpu as pltpu
from jax.sharding import PartitionSpec as P

MESH = pl.DeviceIdType.MESH
LANES = 128
GROUP = 8
CHUNKS = 8
PIECE = 3


def spectral_tables(steps):
    length = 2 * steps
    freqs = steps + 1
    times = lax.broadcasted_iota(jnp.int32, (steps, freqs), 0)
    bins = lax.broadcasted_iota(jnp.int32, (steps, freqs), 1)
    phase = 2.0 * math.pi / length * (times * bins % length).astype(jnp.float32)
    forward = jnp.concatenate([jnp.cos(phase), -jnp.sin(phase)], axis=1)
    weight = jnp.where((bins == 0) | (bins == steps), 1.0, 2.0) / length
    backward = jnp.concatenate([(weight * jnp.cos(phase)).T, (-weight * jnp.sin(phase)).T], axis=0)
    return (forward, backward)


def to_spectrum(series, forward):
    vectors, sensors, steps = series.shape
    flat = jnp.dot(
        series.reshape(vectors * sensors, steps),
        forward,
        precision=lax.Precision.HIGHEST,
        preferred_element_type=jnp.float32,
    )
    return flat.reshape(vectors, sensors, forward.shape[1])


def contract(kernel, spectrum):
    return jnp.einsum(
        "spf,rsf->rpf",
        kernel,
        spectrum,
        precision=lax.Precision.HIGHEST,
        preferred_element_type=jnp.float32,
    )


def general_body(data, spectra):
    steps = data.shape[2]
    freqs = steps + 1
    forward, backward = spectral_tables(steps)
    whole = to_spectrum(lax.all_gather(data, "param", axis=1, tiled=True), forward)
    real_part = whole[..., :freqs]
    imag_part = whole[..., freqs:]
    kernel_re = spectra[0]
    kernel_im = spectra[1]
    out_re = contract(kernel_re, real_part) + contract(kernel_im, imag_part)
    out_im = contract(kernel_re, imag_part) - contract(kernel_im, real_part)
    vectors, points = (out_re.shape[0], out_re.shape[1])
    stacked = jnp.concatenate([out_re, out_im], axis=2).reshape(vectors * points, 2 * freqs)
    partial_field = jnp.dot(
        stacked, backward, precision=lax.Precision.HIGHEST, preferred_element_type=jnp.float32
    ).reshape(vectors, points, steps)
    count = points * lax.axis_size("param") * steps
    share = lax.psum_scatter(partial_field, "sensor", scatter_dimension=0, tiled=True)
    squares = lax.psum(jnp.sum(share * share, axis=(1, 2)), "param")
    scale = jnp.sqrt(squares / count + 1e-06)
    normalized = share / scale[:, None, None]
    gradient, rms_all = (
        lax.all_gather(normalized, "sensor", axis=0, tiled=True),
        lax.all_gather(scale, "sensor", axis=0, tiled=True),
    )
    return (gradient, rms_all)


def split(value):
    high = value.astype(jnp.bfloat16)
    return high, (value - high.astype(jnp.float32)).astype(jnp.bfloat16)


NT_DIMS = (((1,), (1,)), ((), ()))


def product(left, right, dims):
    dot = functools.partial(lax.dot_general, dimension_numbers=dims, preferred_element_type=jnp.float32)
    size = left[0].shape[0]
    both = dot(jnp.concatenate(left, axis=0), right[0])
    return both[:size] + (both[size:] + dot(left[0], right[1]))


def split_product(table, rows, right):
    dot = functools.partial(lax.dot_general, dimension_numbers=NT_DIMS, preferred_element_type=jnp.float32)
    half = table.shape[0] // 2
    both = dot(table, right[0])
    return both[:rows] + (both[half : half + rows] + dot(table[:half], right[1])[:rows])


def folded_layout_fits(steps):
    half = steps // 2
    rest = half + 1 - LANES
    groups = -(-(steps + 1) // (2 * GROUP))
    fits = steps % 2 == 0 and 0 < rest < LANES and half - LANES - (LANES - rest) <= LANES - rest
    return fits and groups % PIECE == 0


def frequency_order(freqs, groups):
    bins = np.arange(groups * 2 * GROUP).reshape(groups, 2, GROUP)
    return [bins[:, core].reshape(-1) for core in range(2)]


def lane_times(steps):
    half = steps // 2
    rest = half + 1 - LANES
    room = LANES - rest
    lane = np.arange(LANES)
    first = np.where(lane < rest, LANES + lane, -1)
    first_odd = np.where(lane < rest - 1, LANES + lane, -1)
    second = np.where(lane >= room, LANES + lane - room, -1)
    tail_a = np.where(lane >= rest, LANES + lane - rest, -1)
    tail_b = np.where(lane < rest - 1 - room, LANES + room + lane, -1)
    return lane, first, first_odd, second, tail_a, tail_b


def fold_maps(steps):
    lane, first, first_odd, second, tail_a, tail_b = lane_times(steps)
    shared = np.where(second >= 0, second, tail_b)
    even = np.concatenate([lane, lane, first, first_odd])
    odd = np.concatenate([lane, lane, tail_a, shared])
    ones = np.ones(LANES, np.int64)
    even_sign = np.concatenate([ones, -ones, ones, -ones])
    odd_sign = np.concatenate([ones, -ones, -ones, np.where(second >= 0, 1, -1)])
    maps = np.full((8, 4 * LANES), -1, np.int32)
    for index, (time, sign) in enumerate(((even, even_sign), (odd, odd_sign))):
        mirror = np.where((time > 0) & (2 * time != steps), steps - time, -1)
        maps[3 * index] = time
        maps[3 * index + 1] = np.where(time < 0, -1, mirror)
        maps[3 * index + 2] = sign
    return maps


def halves(values):
    high = values.astype(jnp.bfloat16)
    return high, (values - high.astype(np.float32)).astype(jnp.bfloat16)


def paired_tables(steps, freqs, groups, rows_pad, wide):
    half = steps // 2
    lane, first, first_odd, second, tail_a, tail_b = lane_times(steps)
    tail = np.where(tail_a >= 0, tail_a, tail_b)
    forward, backward = [], []
    for bins in frequency_order(freqs, groups):
        count = bins.shape[0]
        known = (bins < freqs)[:, None]
        even = (bins % 2 == 0)[:, None]
        angle = bins[:, None] * np.arange(steps)[None, :] % (2 * steps)
        phase = np.pi / steps * angle
        sine = np.where(angle % steps == 0, 0.0, np.sin(phase))
        cosine = np.cos(phase)
        symmetric = np.where(known, np.where(even, cosine, -sine), 0.0)
        other = np.where(known, np.where(even, -sine, cosine), 0.0)
        blocks = []
        for table, times in (
            (symmetric, lane), (other, lane), (symmetric, first), (other, first_odd), (symmetric, second), (other, tail),
        ):
            limit = half if table is symmetric else half - 1
            inside = (times >= 0) & (times <= limit)
            value = np.where(inside[None, :], table[:, np.clip(times, 0, limit)], 0.0).astype(np.float32)
            block = np.zeros((2, rows_pad, LANES), jnp.bfloat16)
            block[0, :count], block[1, :count] = halves(value)
            blocks.append(block.reshape(2 * rows_pad, LANES))
        forward.append(np.stack(blocks))
        weight = np.where((bins == 0) | (bins == steps), 0.5, 1.0)[:, None] / steps
        inverse = np.zeros((2, 2, rows_pad, wide), jnp.bfloat16)
        for position, table in enumerate((symmetric, other)):
            value = (table * weight).astype(np.float32)
            inverse[0, position, :count, :steps], inverse[1, position, :count, :steps] = halves(value)
        backward.append(inverse)
    return np.stack(forward), np.stack(backward)


def kernel(
    n, lines, vectors, local, steps, points, freqs, groups, wide,
    data_ref, spectra_ref, forward_ref, backward_ref, maps_ref,
    out_ref, rms_ref,
    series, fold, raw, packed, kbuf, gathered, table, inverse, spectrum, product_s, own_val, send_val, recv_val,
    partial, pair, square, squares,
    load_sem, raw_sem, k_send, k_recv, z_send, z_recv, y_send, y_recv, c_send, c_recv, w_send, w_recv,
    v_send, v_recv, f_send, f_recv, r_send, r_recv,
):
    me = lax.axis_index("param")
    core = lax.axis_index("sensor")
    x = lax.rem(me, 2)
    y = lax.rem(me // 2, 2)
    z = me // 4
    plane = 4
    other_chip = me + 1 - 2 * x
    y_chip = me + 2 - 4 * y
    other_core = 1 - core
    z_mate = z + 1 - 2 * lax.rem(z, 2)
    half = steps // 2
    rest = half + 1 - LANES
    rows = points * GROUP
    count = groups * GROUP
    pieces = groups // PIECE
    span = PIECE * 2 * GROUP

    barrier = pltpu.get_barrier_semaphore()

    @pl.loop(1, n)
    def _(step):
        pl.semaphore_signal(barrier, inc=1, device_id=(lax.rem(me + step, n), core), device_id_type=MESH)

    pl.semaphore_signal(barrier, inc=1, device_id=(me, other_core), device_id_type=MESH)
    pl.semaphore_signal(barrier, inc=1, device_id=(other_chip, other_core), device_id_type=MESH)

    def raw_copy(piece):
        begin = piece * span
        size = min(span, freqs - begin)
        return pltpu.make_async_copy(
            spectra_ref.at[:, pl.ds(begin, size)], raw.at[:, pl.ds(begin, size)], raw_sem.at[piece]
        )

    data_copy = pltpu.make_async_copy(data_ref, series, load_sem.at[0])
    forward_copy = pltpu.make_async_copy(forward_ref.at[core], table, load_sem.at[1])
    backward_copy = pltpu.make_async_copy(
        backward_ref.at[core], inverse.at[:, :, pl.ds(0, backward_ref.shape[3])], load_sem.at[2]
    )
    raw_copy(0).start()
    data_copy.start()
    for piece in range(1, pieces):
        raw_copy(piece).start()
    forward_copy.start()
    backward_copy.start()

    raw[:, freqs:] = jnp.zeros((2, raw.shape[1] - freqs) + tuple(raw.shape[2:]), jnp.float32)
    pad = inverse.shape[2] - backward_ref.shape[3]
    inverse[:, :, inverse.shape[2] - pad :, :] = jnp.zeros((2, 2, pad, wide), jnp.bfloat16)
    own_val[count:, :] = jnp.zeros((own_val.shape[0] - count, LANES), jnp.float32)

    strip = 64

    @pl.loop(0, fold.shape[1] // strip)
    def _(part):
        begin = pl.multiple_of(part * strip, strip)
        time = lax.broadcasted_iota(jnp.int32, (strip, 4 * LANES), 0) + begin
        for side in range(2):
            direct = jnp.where(time == maps_ref[3 * side : 3 * side + 1, :], 1.0, 0.0)
            sign = maps_ref[3 * side + 2 : 3 * side + 3, :].astype(jnp.float32)
            mirror = jnp.where(time == maps_ref[3 * side + 1 : 3 * side + 2, :], sign, 0.0)
            fold[side, pl.ds(begin, strip), :] = (direct + mirror).astype(jnp.bfloat16)

    upper = lax.broadcasted_iota(jnp.int32, (8, LANES), 0) < points
    stripe = lax.broadcasted_iota(jnp.int32, (8, LANES), 1) // local % 2 == 0

    def sort_piece(piece):
        @pl.loop(0, 2)
        def _(part):
            @pl.loop(piece * PIECE, (piece + 1) * PIECE)
            def _(group):
                for side in range(2):
                    for duo in range(GROUP // 2):
                        begin = group * 2 * GROUP + side * GROUP + 2 * duo
                        first = raw[part, begin]
                        second = raw[part, begin + 1]
                        low = jnp.where(upper, first, pltpu.roll(second, points, 0))
                        high = jnp.where(upper, pltpu.roll(first, points, 0), second)
                        packed[0, part, group, side, duo] = jnp.where(stripe, low, pltpu.roll(high, local, 1))
                        packed[1, part, group, side, duo] = jnp.where(stripe, pltpu.roll(high, LANES - local, 1), low)

    def k_copy(piece, target):
        begin = piece * PIECE
        rel = core if target == 0 else other_core
        return pltpu.make_async_remote_copy(
            src_ref=packed.at[1 - x, :, pl.ds(begin, PIECE), target],
            dst_ref=kbuf.at[1 + rel, :, pl.ds(begin, PIECE)],
            send_sem=k_send.at[piece, target], recv_sem=k_recv.at[piece, 1 + rel],
            device_id=(other_chip, target), device_id_type=MESH,
        )

    def k_keep(piece):
        begin = piece * PIECE
        return pltpu.make_async_remote_copy(
            src_ref=packed.at[x, :, pl.ds(begin, PIECE), other_core],
            dst_ref=kbuf.at[0, :, pl.ds(begin, PIECE)],
            send_sem=k_send.at[piece, 2], recv_sem=k_recv.at[piece, 0],
            device_id=(me, other_core), device_id_type=MESH,
        )

    def k_arrival(piece, slot):
        begin = piece * PIECE
        return pltpu.make_async_remote_copy(
            src_ref=packed.at[0, :, pl.ds(begin, PIECE), 0],
            dst_ref=kbuf.at[slot, :, pl.ds(begin, PIECE)],
            send_sem=k_send.at[piece, 2], recv_sem=k_recv.at[piece, slot],
            device_id=(me, other_core), device_id_type=MESH,
        )

    def send_piece(piece):
        for target in range(2):
            k_copy(piece, target).start()
        k_keep(piece).start()

    raw_copy(0).wait()
    sort_piece(0)
    pl.semaphore_wait(barrier, n + 1)
    send_piece(0)

    def slot(line, row, column):
        return line * plane + row * 2 + column

    def place(line, row):
        upper_line = line // 2
        return lax.rem(line, 2) * plane + row * 2 + upper_line + x - 2 * upper_line * x

    def block(chunk, line, row, rel=0):
        position = rel * (n // 2) + place(line, row)
        return gathered.at[chunk, pl.ds(pl.multiple_of(position * local, local), local), :]

    data_copy.wait()
    plain = (((1,), (0,)), ((), ()))
    folded = []
    for side in range(2):
        values = jnp.concatenate([series[2 * chunk + side] for chunk in range(CHUNKS)], axis=0)
        high = values.astype(jnp.bfloat16)
        left = values - high.astype(jnp.float32)
        middle = left.astype(jnp.bfloat16)
        low = (left - middle.astype(jnp.float32)).astype(jnp.bfloat16)
        result = lax.dot_general(
            jnp.concatenate([high, middle, low], axis=0), fold[side, :steps, :], plain,
            preferred_element_type=jnp.float32,
        )
        size = CHUNKS * local
        folded.append(result[:size] + (result[size : 2 * size] + result[2 * size :]))
    own_row = pl.ds(pl.multiple_of(place(z, y) * local, local), local)
    for chunk in range(CHUNKS):
        even = folded[0][chunk * local : (chunk + 1) * local]
        odd = folded[1][chunk * local : (chunk + 1) * local]
        gathered[chunk, own_row, 0 : 2 * LANES] = even[:, : 2 * LANES]
        gathered[chunk, own_row, 2 * LANES : 4 * LANES] = odd[:, : 2 * LANES]
        gathered[chunk, own_row, 4 * LANES : 5 * LANES] = (
            even[:, 2 * LANES : 3 * LANES] + odd[:, 2 * LANES : 3 * LANES]
        )
        gathered[chunk, own_row, 5 * LANES : 6 * LANES] = even[:, 3 * LANES :]
        gathered[chunk, own_row, 6 * LANES :] = odd[:, 3 * LANES :]

    def send(source, target, send_sem, recv_sem):
        return pltpu.make_async_remote_copy(
            src_ref=source, dst_ref=source, send_sem=send_sem, recv_sem=recv_sem,
            device_id=target, device_id_type=MESH,
        )

    def line_copy(chunk, step, way):
        source = jnp.clip(z - way * step, 0, lines - 1)
        target = jnp.clip(z + way, 0, lines - 1)
        index = step if way > 0 else lines + step
        return send(
            block(chunk, source, y), (slot(target, y, x), core), z_send.at[chunk, index], z_recv.at[chunk, index]
        )

    def line_arrival(chunk, step, way):
        source = jnp.clip(z - way * (step + 1), 0, lines - 1)
        target = jnp.clip(z + way, 0, lines - 1)
        index = step if way > 0 else lines + step
        return source, send(
            block(chunk, source, y), (slot(target, y, x), core), z_send.at[chunk, index], z_recv.at[chunk, index]
        )

    def sends(step, way):
        inside = z + 1 < lines if way > 0 else z > 0
        begun = z >= step if way > 0 else z + step < lines
        return jnp.logical_and(inside, begun)

    def receives(step, way):
        return z >= step + 1 if way > 0 else z + step + 1 < lines

    def y_copy(chunk, line):
        return send(block(chunk, line, y), (y_chip, core), y_send.at[chunk, line], y_recv.at[chunk, line])

    def y_arrival(chunk, line):
        return send(block(chunk, line, 1 - y), (y_chip, core), y_send.at[chunk, line], y_recv.at[chunk, line])

    def turn_copy(chunk):
        return send(block(chunk, z, 1 - y), (slot(z_mate, y, x), core), w_send.at[chunk], w_recv.at[chunk])

    def turn_arrival(chunk):
        return send(block(chunk, z_mate, 1 - y), (slot(z_mate, y, x), core), w_send.at[chunk], w_recv.at[chunk])

    def turns(chunk):
        return lax.rem(chunk, 2) == 0

    def by_row(chunk, line):
        return jnp.logical_not(jnp.logical_and(turns(chunk), line == z_mate))

    def core_copy(chunk, row, line):
        index = row * lines + line
        return pltpu.make_async_remote_copy(
            src_ref=block(chunk, line, row), dst_ref=block(chunk, line, row, 1),
            send_sem=c_send.at[chunk, index], recv_sem=c_recv.at[chunk, index],
            device_id=(me, other_core), device_id_type=MESH,
        )

    def start_lines(chunk):
        for way in (1, -1):

            @pl.when(sends(0, way))
            def _():
                line_copy(chunk, 0, way).start()

        y_copy(chunk, z).start()
        core_copy(chunk, y, z).start()

    def from_lines(chunk, step):
        for way in (1, -1):

            @pl.when(receives(step, way))
            def _():
                source, arrival = line_arrival(chunk, step, way)
                arrival.wait_recv()
                if step + 1 < lines - 1:

                    @pl.when(sends(step + 1, way))
                    def _():
                        line_copy(chunk, step + 1, way).start()

                @pl.when(by_row(chunk, source))
                def _():
                    y_copy(chunk, source).start()

                core_copy(chunk, y, source).start()

    def from_mate(chunk):
        y_arrival(chunk, z).wait_recv()

        @pl.when(turns(chunk))
        def _():
            turn_copy(chunk).start()

        core_copy(chunk, 1 - y, z).start()

    def from_row(chunk):
        for step in range(1, lines):
            line = lax.rem(z + step, lines)

            @pl.when(by_row(chunk, line))
            def _():
                y_arrival(chunk, line).wait_recv()

            @pl.when(jnp.logical_not(by_row(chunk, line)))
            def _():
                turn_arrival(chunk).wait_recv()

            core_copy(chunk, 1 - y, line).start()

    def from_core(chunk):
        for line in range(lines):
            for row in range(2):
                core_copy(chunk, row, line).wait_recv()

    lane_index = lax.broadcasted_iota(jnp.int32, (gathered.shape[1], LANES), 1)

    def transform(chunk):
        def lanes(index):
            return gathered[chunk, :, index * LANES : (index + 1) * LANES]

        for which in range(4):
            odd = which // 2
            position = which % 2
            if which < 2:
                tail = lanes(4 + which)
            elif which == 2:
                tail = lanes(6)
            else:
                tail = jnp.where(lane_index >= rest, lanes(4), lanes(6))
            right = split(jnp.concatenate([lanes(which), tail], axis=1))
            left = jnp.concatenate([table[position], table[2 + which]], axis=1)
            result = split_product(left, count, right)
            for lane in range(2):
                spectrum[lane, pl.ds(position * vectors + 2 * chunk + odd, count, stride=2 * vectors), :] = result[
                    :, lane * LANES : (lane + 1) * LANES
                ]

    pl.loop(0, CHUNKS)(start_lines)

    for piece in range(1, pieces):
        raw_copy(piece).wait()
        sort_piece(piece)
        send_piece(piece)

    forward_copy.wait()
    backward_copy.wait()

    def finish(chunk):
        from_core(chunk)
        transform(chunk)

    stages = [
        (functools.partial(from_lines, step=0), 0), (from_mate, 0),
        (functools.partial(from_lines, step=1), 1), (functools.partial(from_lines, step=2), 2),
        (from_row, 3), (finish, 4),
    ]

    @pl.loop(0, CHUNKS + 4)
    def _(turn):
        for stage, age in stages:
            chunk = turn - age

            @pl.when(jnp.logical_and(chunk >= 0, chunk < CHUNKS))
            def _():
                stage(chunk)

    columns = GROUP * 2 * vectors
    row_freq = lax.broadcasted_iota(jnp.int32, (4 * rows, columns), 0) // points % GROUP
    col_freq = lax.broadcasted_iota(jnp.int32, (4 * rows, columns), 1) // (2 * vectors)
    own = row_freq == col_freq
    lane = lax.broadcasted_iota(jnp.int32, (2 * rows, LANES), 1)
    row = lax.broadcasted_iota(jnp.int32, (2 * rows, LANES), 0) // points % 2
    sign = jnp.where((lane % (2 * vectors) < vectors) == (row == 0), 1.0, -1.0)
    step_rows = PIECE * GROUP
    owner_lane = lax.broadcasted_iota(jnp.int32, (step_rows, LANES), 1) // (2 * vectors)

    def value_copy(piece):
        place_rows = pl.ds(pl.multiple_of(piece * step_rows, GROUP), step_rows)
        return pltpu.make_async_remote_copy(
            src_ref=send_val.at[place_rows], dst_ref=recv_val.at[place_rows],
            send_sem=v_send.at[piece], recv_sem=v_recv.at[piece],
            device_id=(other_chip, core), device_id_type=MESH,
        )

    @pl.loop(0, pieces)
    def _(piece):
        for arrival in range(3):
            k_arrival(piece, arrival).wait_recv()
        for step in range(PIECE):
            group = piece * PIECE + step
            begin = pl.multiple_of(group * columns, columns)
            right = split(
                jnp.concatenate([spectrum[0, pl.ds(begin, columns), :], spectrum[1, pl.ds(begin, columns), :]], axis=1)
            )
            parts = []
            for part in range(2):
                for near, far in (
                    (packed[x, part, group, core], kbuf[0, part, group]), (kbuf[1, part, group], kbuf[2, part, group]),
                ):
                    parts.append(jnp.concatenate([near.reshape(rows, LANES), far.reshape(rows, LANES)], axis=1))
            left = jnp.concatenate(parts, axis=0)
            found = jnp.where(own, product(split(left), right, NT_DIMS), 0.0)
            width = columns
            while width > LANES:
                width //= 2
                found = found[:, :width] + found[:, width:]
            hop = LANES // 2
            while hop >= 2 * vectors:
                found = found + pltpu.roll(found, hop, 1)
                hop //= 2
            value = found[: 2 * rows] + sign * pltpu.roll(found[2 * rows :], vectors, 1)
            for owner in range(2):
                product_s[owner, pl.ds(pl.multiple_of(group * rows, rows), rows), :] = value[
                    owner * rows : (owner + 1) * rows
                ]
        begin = piece * PIECE * rows
        for owner, target in ((1, send_val), (0, own_val)):
            merged = jnp.zeros((step_rows, LANES), jnp.float32)
            for point in range(points):
                merged = jnp.where(
                    owner_lane == point, product_s[owner, pl.ds(begin + point, step_rows, stride=points), :], merged
                )
            target[pl.ds(pl.multiple_of(piece * step_rows, GROUP), step_rows), :] = merged
        value_copy(piece).start()

    @pl.loop(0, pieces)
    def _(piece):
        value_copy(piece).wait_recv()

    own_val[:count, :] = own_val[:count, :] + recv_val[...]
    turned = own_val[...].T
    by_position = []
    for position in range(2):
        by_position.append(jnp.concatenate(
            [turned[(2 * point + position) * vectors : (2 * point + position + 1) * vectors] for point in range(points)],
            axis=0,
        ))
    left = split(jnp.concatenate(by_position, axis=1))
    deep = 2 * inverse.shape[2]
    partial[...] = product(left, (inverse[0].reshape(deep, wide), inverse[1].reshape(deep, wide)), plain)

    field_copy = pltpu.make_async_remote_copy(
        src_ref=partial, dst_ref=pair, send_sem=f_send.at[0], recv_sem=f_recv.at[0],
        device_id=(me, other_core), device_id_type=MESH,
    )
    field_copy.start()
    field_copy.wait_recv()

    total = partial[...] + pair[...]
    energy = total * total
    summed = energy[:vectors]
    for point in range(1, points):
        summed = summed + energy[point * vectors : (point + 1) * vectors]
    diagonal = lax.broadcasted_iota(jnp.int32, (vectors, LANES), 0) == lax.broadcasted_iota(
        jnp.int32, (vectors, LANES), 1
    )
    column = jnp.sum(summed, axis=1, keepdims=True)
    flat = jnp.sum(jnp.where(diagonal, column, 0.0), axis=0, keepdims=True)
    flat = jnp.broadcast_to(flat, (8, LANES))
    square[...] = flat
    squares[me] = flat

    def square_copy(step):
        return pltpu.make_async_remote_copy(
            src_ref=square, dst_ref=squares.at[me], send_sem=r_send.at[step], recv_sem=r_recv.at[step],
            device_id=(lax.rem(me + step, n), core), device_id_type=MESH,
        )

    def square_arrival(step):
        return pltpu.make_async_remote_copy(
            src_ref=square, dst_ref=squares.at[lax.rem(me + n - step, n)],
            send_sem=r_send.at[step], recv_sem=r_recv.at[step],
            device_id=(lax.rem(me + step, n), core), device_id_type=MESH,
        )

    @pl.loop(1, n)
    def _(step):
        square_copy(step).start()

    @pl.loop(0, CHUNKS)
    def _(chunk):
        for step in range(lines - 1):
            for way in (1, -1):

                @pl.when(sends(step, way))
                def _():
                    line_copy(chunk, step, way).wait_send()

        for line in range(lines):

            @pl.when(by_row(chunk, line))
            def _():
                y_copy(chunk, line).wait_send()

            for row in range(2):
                core_copy(chunk, row, line).wait_send()

        @pl.when(turns(chunk))
        def _():
            turn_copy(chunk).wait_send()

    for piece in range(pieces):
        for target in range(2):
            k_copy(piece, target).wait_send()
        k_keep(piece).wait_send()
        value_copy(piece).wait_send()
    field_copy.wait_send()

    @pl.loop(1, n)
    def _(step):
        square_arrival(step).wait()

    energy_all = squares[0]
    for device in range(1, n):
        energy_all = energy_all + squares[device]
    scale = jnp.sqrt(energy_all / (points * n * steps) + 1e-06)
    rms_ref[...] = scale
    spread = jnp.broadcast_to(scale[:1], (vectors, LANES))
    divisor = jnp.sum(jnp.where(diagonal, spread, 0.0), axis=1, keepdims=True)
    for point in range(points):
        out_ref[point] = total[point * vectors : (point + 1) * vectors, :steps] / divisor


def paired_body(data, spectra):
    n = lax.axis_size("param")
    vectors, local, steps = data.shape
    sensors, points, freqs = spectra.shape[1:]
    wide = -(-steps // LANES) * LANES
    groups = -(-freqs // (2 * GROUP))
    count = groups * GROUP
    rows_pad = -(-count // 16) * 16
    deep = -(-count // LANES) * LANES
    pieces = groups // PIECE
    lines = n // 4
    forward, backward = paired_tables(steps, freqs, groups, rows_pad, wide)
    maps = fold_maps(steps)

    turned = jnp.transpose(spectra, (0, 3, 2, 1)).reshape(2, freqs, points, 2, LANES)
    turned = jnp.transpose(turned, (0, 1, 3, 2, 4)).reshape(2, freqs, 2 * points, LANES)

    hbm = pl.BlockSpec(memory_space=pl.ANY)
    vmem = pl.BlockSpec(memory_space=pltpu.VMEM)
    dma = pltpu.SemaphoreType.DMA
    f32, bf16 = jnp.float32, jnp.bfloat16
    fields, scale = pl.pallas_call(
        functools.partial(kernel, n, lines, vectors, local, steps, points, freqs, groups, wide),
        out_shape=(
            jax.ShapeDtypeStruct((points, vectors, steps), f32),
            jax.ShapeDtypeStruct((8, LANES), f32),
        ),
        in_specs=[hbm, hbm, hbm, hbm, vmem],
        out_specs=(vmem, vmem),
        scratch_shapes=[
            pltpu.VMEM((vectors, local, steps), f32),
            pltpu.VMEM((2, wide, 4 * LANES), bf16),
            pltpu.VMEM((2, 2 * count, 2 * points, LANES), f32),
            pltpu.VMEM((2, 2, groups, 2, GROUP // 2, 2 * points, LANES), f32),
            pltpu.VMEM((3, 2, groups, GROUP // 2, 2 * points, LANES), f32),
            pltpu.VMEM((CHUNKS, sensors, 7 * LANES), f32),
            pltpu.VMEM((6, 2 * rows_pad, LANES), bf16),
            pltpu.VMEM((2, 2, deep, wide), bf16),
            pltpu.VMEM((2, count * 2 * vectors, LANES), f32),
            pltpu.VMEM((2, count * points, LANES), f32),
            pltpu.VMEM((deep, LANES), f32),
            pltpu.VMEM((count, LANES), f32),
            pltpu.VMEM((count, LANES), f32),
            pltpu.VMEM((points * vectors, wide), f32),
            pltpu.VMEM((points * vectors, wide), f32),
            pltpu.VMEM((8, LANES), f32),
            pltpu.VMEM((n, 8, LANES), f32),
            dma((3,)),
            dma((pieces,)),
            dma((pieces, 3)), dma((pieces, 3)),
            dma((CHUNKS, 2 * lines)), dma((CHUNKS, 2 * lines)),
            dma((CHUNKS, lines)), dma((CHUNKS, lines)),
            dma((CHUNKS, 2 * lines)), dma((CHUNKS, 2 * lines)),
            dma((CHUNKS,)), dma((CHUNKS,)),
            dma((pieces,)), dma((pieces,)),
            dma((1,)), dma((1,)),
            dma((n,)), dma((n,)),
        ],
        compiler_params=pltpu.CompilerParams(
            collective_id=0, has_side_effects=True, vmem_limit_bytes=60 * 1024 * 1024
        ),
    )(data, turned, jnp.asarray(forward), jnp.asarray(backward), jnp.asarray(maps))
    return (jnp.transpose(fields, (1, 0, 2)), scale[0, :vectors])


def solution(mesh):
    in_specs = (P(None, ("sensor", "param"), None), P(None, "sensor", "param", None))
    out_specs = (P(None, "param", None), P())
    n = mesh.shape["param"]
    pair = mesh.shape["sensor"] == 2 and n == 16

    def body(data, spectra):
        vectors, local, _ = data.shape
        sensors, points = spectra.shape[1:3]
        fits = local * n * 2 == 2 * sensors and sensors == 2 * LANES and vectors == 2 * CHUNKS
        fits = fits and points * 2 * vectors == LANES and folded_layout_fits(data.shape[2])
        return (paired_body if pair and fits else general_body)(data, spectra)

    return jax.shard_map(body, mesh=mesh, in_specs=in_specs, out_specs=out_specs, check_vma=False)
```

time: 95.4 us -> 73.4 us (0.77)
  Pallas kernels: 88.7 us -> 69.6 us
  local copies, waits for them, and re-layouts: 4.04 us -> 2.84 us
    pallas_call x1, Pallas kernels: 88.7 us -> 69.6 us  [paired_body(): pl.pallas_call(functools.partial(kernel, n, lines, vectors, local, steps,...]
    slice x1 -> x0, local copies, waits for them, and re-layouts: 1.32 us -> none  [paired_body(): return (jnp.transpose(fields, (1, 0, 2)), scale[:, 0])]
where the time goes in v1:
time: 73.4 us; the launch traced here: 73.1 us
  Pallas kernels  69.6 us (95%)
  local copies, waits for them, and re-layouts  2.84 us (4%)
    pallas_call x1, Pallas kernels, paired_body(): pl.pallas_call(functools.partial(kernel, n, lines, vectors, local, steps,...  69.6 us
    unnamed x1, local copies, waits for them, and re-layouts  1.65 us

profile of v1, /device:TPU:0, one launch (start us, length us, event | category | flops | bytes accessed | tf_op | source)
XLA Modules:
  0.0 73.1 jit_solution(2230264560217775865)
XLA Ops:
  0.6 69.6 %shard_map.68 = (f32[4,16,420]{2,1,0:T(8,128)}, f32[8,128]{1,0:T(8,128)}) custom-call(f32[16,16,420]{2,1,0:T(8,128)} %data_ref.1, f32[2,421,8,128]{3,2,1,0:T(8,128)} %bitcast.10, bf16[2,6,448,128]{3,2,1,0:T(8,128)(2,1)} %constant.6.clone.forward_ref, bf16[2,2,2,224,512]{4,3,2,1,0:T(8,128)(2,1)} %constant.7.clone.backward_ref, s32[8,512]{1,0:T(8,128)} %constant.8.clone.maps_ref), custom_call_target="tpu_custom_call" | custom-call | tf_op jit(solution)/shard_map/pallas_call | solution.py:693
  70.3 1.6 %copy.8 = f32[16,4,420]{2,1,0:T(4,128)} copy(f32[16,4,420]{2,0,1:T(8,128)} %bitcast.11) | data formatting | bytes 215040
  71.9 1.2 %slice_bitcast_fusion = f32[16]{0:T(128)} fusion(f32[8,128]{1,0:T(8,128)} %get-tuple-element.5), kind=kLoop, calls=%fused_computation | loop fusion | bytes 128 | tf_op jit(solution)/shard_map/squeeze | solution.py:734

commit v2 on v1

--- a/solution.py
+++ b/solution.py
@@ -14,6 +14,7 @@
 GROUP = 8
 CHUNKS = 8
 PIECE = 3
+BATCHES = 3
 
 
 def spectral_tables(steps):
@@ -104,7 +105,7 @@
     rest = half + 1 - LANES
     groups = -(-(steps + 1) // (2 * GROUP))
     fits = steps % 2 == 0 and 0 < rest < LANES and half - LANES - (LANES - rest) <= LANES - rest
-    return fits and groups % PIECE == 0
+    return fits and groups % (PIECE * BATCHES) == 0
 
 
 def frequency_order(freqs, groups):
@@ -210,12 +211,20 @@
 
     barrier = pltpu.get_barrier_semaphore()
 
-    @pl.loop(1, n)
-    def _(step):
-        pl.semaphore_signal(barrier, inc=1, device_id=(lax.rem(me + step, n), core), device_id_type=MESH)
-
-    pl.semaphore_signal(barrier, inc=1, device_id=(me, other_core), device_id_type=MESH)
-    pl.semaphore_signal(barrier, inc=1, device_id=(other_chip, other_core), device_id_type=MESH)
+    for neighbour in ((other_chip, core), (other_chip, other_core), (y_chip, core), (me, other_core)):
+        pl.semaphore_signal(barrier, inc=1, device_id=neighbour, device_id_type=MESH)
+
+    @pl.when(z > 0)
+    def _():
+        pl.semaphore_signal(barrier, inc=1, device_id=(me - plane, core), device_id_type=MESH)
+
+    @pl.when(z + 1 < lines)
+    def _():
+        pl.semaphore_signal(barrier, inc=1, device_id=(me + plane, core), device_id_type=MESH)
+
+    def filled(piece, target):
+        known = -(-(freqs - target * GROUP) // (2 * GROUP))
+        return min(PIECE, known - piece * PIECE)
 
     def raw_copy(piece):
         begin = piece * span
@@ -239,6 +248,15 @@
     raw[:, freqs:] = jnp.zeros((2, raw.shape[1] - freqs) + tuple(raw.shape[2:]), jnp.float32)
     pad = inverse.shape[2] - backward_ref.shape[3]
     inverse[:, :, inverse.shape[2] - pad :, :] = jnp.zeros((2, 2, pad, wide), jnp.bfloat16)
+    short = filled(pieces - 1, 1)
+    if short < PIECE:
+
+        @pl.when(core == 1)
+        def _():
+            begin = (pieces - 1) * PIECE + short
+            for owner in range(1, 3):
+                kbuf[owner, :, begin:] = jnp.zeros((2, PIECE - short) + tuple(kbuf.shape[3:]), jnp.float32)
+
     own_val[count:, :] = jnp.zeros((own_val.shape[0] - count, LANES), jnp.float32)
 
     strip = 64
@@ -273,10 +291,11 @@
 
     def k_copy(piece, target):
         begin = piece * PIECE
+        size = filled(piece, target)
         rel = core if target == 0 else other_core
         return pltpu.make_async_remote_copy(
-            src_ref=packed.at[1 - x, :, pl.ds(begin, PIECE), target],
-            dst_ref=kbuf.at[1 + rel, :, pl.ds(begin, PIECE)],
+            src_ref=packed.at[1 - x, :, pl.ds(begin, size), target],
+            dst_ref=kbuf.at[1 + rel, :, pl.ds(begin, size)],
             send_sem=k_send.at[piece, target], recv_sem=k_recv.at[piece, 1 + rel],
             device_id=(other_chip, target), device_id_type=MESH,
         )
@@ -290,14 +309,23 @@
             device_id=(me, other_core), device_id_type=MESH,
         )
 
-    def k_arrival(piece, slot):
+    def k_arrival(piece, slot, size):
         begin = piece * PIECE
         return pltpu.make_async_remote_copy(
-            src_ref=packed.at[0, :, pl.ds(begin, PIECE), 0],
-            dst_ref=kbuf.at[slot, :, pl.ds(begin, PIECE)],
+            src_ref=packed.at[0, :, pl.ds(begin, size), 0],
+            dst_ref=kbuf.at[slot, :, pl.ds(begin, size)],
             send_sem=k_send.at[piece, 2], recv_sem=k_recv.at[piece, slot],
             device_id=(me, other_core), device_id_type=MESH,
         )
+
+    def wait_piece(piece):
+        k_arrival(piece, 0, PIECE).wait_recv()
+        for target in range(2):
+
+            @pl.when(core == target)
+            def _():
+                for arrival in range(1, 3):
+                    k_arrival(piece, arrival, filled(piece, target)).wait_recv()
 
     def send_piece(piece):
         for target in range(2):
@@ -306,7 +334,7 @@
 
     raw_copy(0).wait()
     sort_piece(0)
-    pl.semaphore_wait(barrier, n + 1)
+    pl.semaphore_wait(barrier, 4 + jnp.minimum(z, 1) + jnp.minimum(lines - 1 - z, 1))
     send_piece(0)
 
     def slot(line, row, column):
@@ -390,7 +418,7 @@
         return send(block(chunk, z_mate, 1 - y), (slot(z_mate, y, x), core), w_send.at[chunk], w_recv.at[chunk])
 
     def turns(chunk):
-        return lax.rem(chunk, 2) == 0
+        return chunk >= CHUNKS // 2
 
     def by_row(chunk, line):
         return jnp.logical_not(jnp.logical_and(turns(chunk), line == z_mate))
@@ -434,12 +462,12 @@
 
     def from_mate(chunk):
         y_arrival(chunk, z).wait_recv()
-
+        core_copy(chunk, 1 - y, z).start()
+
+    def to_mate(chunk):
         @pl.when(turns(chunk))
         def _():
             turn_copy(chunk).start()
-
-        core_copy(chunk, 1 - y, z).start()
 
     def from_row(chunk):
         for step in range(1, lines):
@@ -500,10 +528,10 @@
     stages = [
         (functools.partial(from_lines, step=0), 0), (from_mate, 0),
         (functools.partial(from_lines, step=1), 1), (functools.partial(from_lines, step=2), 2),
-        (from_row, 3), (finish, 4),
+        (to_mate, 4), (from_row, 6), (finish, 7),
     ]
 
-    @pl.loop(0, CHUNKS + 4)
+    @pl.loop(0, CHUNKS + 7)
     def _(turn):
         for stage, age in stages:
             chunk = turn - age
@@ -519,23 +547,29 @@
     lane = lax.broadcasted_iota(jnp.int32, (2 * rows, LANES), 1)
     row = lax.broadcasted_iota(jnp.int32, (2 * rows, LANES), 0) // points % 2
     sign = jnp.where((lane % (2 * vectors) < vectors) == (row == 0), 1.0, -1.0)
-    step_rows = PIECE * GROUP
+    batch = groups // BATCHES
+    step_rows = batch * GROUP
     owner_lane = lax.broadcasted_iota(jnp.int32, (step_rows, LANES), 1) // (2 * vectors)
 
-    def value_copy(piece):
-        place_rows = pl.ds(pl.multiple_of(piece * step_rows, GROUP), step_rows)
+    def value_copy(turn):
+        place_rows = pl.ds(pl.multiple_of(turn * step_rows, GROUP), step_rows)
         return pltpu.make_async_remote_copy(
             src_ref=send_val.at[place_rows], dst_ref=recv_val.at[place_rows],
-            send_sem=v_send.at[piece], recv_sem=v_recv.at[piece],
+            send_sem=v_send.at[turn], recv_sem=v_recv.at[turn],
             device_id=(other_chip, core), device_id_type=MESH,
         )
 
-    @pl.loop(0, pieces)
-    def _(piece):
-        for arrival in range(3):
-            k_arrival(piece, arrival).wait_recv()
-        for step in range(PIECE):
-            group = piece * PIECE + step
+    @pl.loop(0, BATCHES)
+    def _(turn):
+        for which in range(BATCHES):
+
+            @pl.when(turn == which)
+            def _():
+                for piece in range(which * batch // PIECE, (which + 1) * batch // PIECE):
+                    wait_piece(piece)
+
+        for step in range(batch):
+            group = turn * batch + step
             begin = pl.multiple_of(group * columns, columns)
             right = split(
                 jnp.concatenate([spectrum[0, pl.ds(begin, columns), :], spectrum[1, pl.ds(begin, columns), :]], axis=1)
@@ -561,19 +595,19 @@
                 product_s[owner, pl.ds(pl.multiple_of(group * rows, rows), rows), :] = value[
                     owner * rows : (owner + 1) * rows
                 ]
-        begin = piece * PIECE * rows
+        begin = turn * batch * rows
         for owner, target in ((1, send_val), (0, own_val)):
             merged = jnp.zeros((step_rows, LANES), jnp.float32)
             for point in range(points):
                 merged = jnp.where(
                     owner_lane == point, product_s[owner, pl.ds(begin + point, step_rows, stride=points), :], merged
                 )
-            target[pl.ds(pl.multiple_of(piece * step_rows, GROUP), step_rows), :] = merged
-        value_copy(piece).start()
-
-    @pl.loop(0, pieces)
-    def _(piece):
-        value_copy(piece).wait_recv()
+            target[pl.ds(pl.multiple_of(turn * step_rows, GROUP), step_rows), :] = merged
+        value_copy(turn).start()
+
+    @pl.loop(0, BATCHES)
+    def _(turn):
+        value_copy(turn).wait_recv()
 
     own_val[:count, :] = own_val[:count, :] + recv_val[...]
     turned = own_val[...].T
@@ -651,7 +685,8 @@
         for target in range(2):
             k_copy(piece, target).wait_send()
         k_keep(piece).wait_send()
-        value_copy(piece).wait_send()
+    for turn in range(BATCHES):
+        value_copy(turn).wait_send()
     field_copy.wait_send()
 
     @pl.loop(1, n)
@@ -663,10 +698,20 @@
         energy_all = energy_all + squares[device]
     scale = jnp.sqrt(energy_all / (points * n * steps) + 1e-06)
     rms_ref[...] = scale
-    spread = jnp.broadcast_to(scale[:1], (vectors, LANES))
+    out_ref[...] = total
+
+
+def finish_kernel(field_ref, scale_ref, out_ref, rms_ref):
+    vectors, points, steps = out_ref.shape
+    scale = scale_ref[:1]
+    rms_ref[...] = scale[0, :vectors]
+    diagonal = lax.broadcasted_iota(jnp.int32, (vectors, LANES), 0) == lax.broadcasted_iota(
+        jnp.int32, (vectors, LANES), 1
+    )
+    spread = jnp.broadcast_to(scale, (vectors, LANES))
     divisor = jnp.sum(jnp.where(diagonal, spread, 0.0), axis=1, keepdims=True)
     for point in range(points):
-        out_ref[point] = total[point * vectors : (point + 1) * vectors, :steps] / divisor
+        out_ref[:, point, :] = field_ref[point * vectors : (point + 1) * vectors, :steps] / divisor
 
 
 def paired_body(data, spectra):
@@ -693,7 +738,7 @@
     fields, scale = pl.pallas_call(
         functools.partial(kernel, n, lines, vectors, local, steps, points, freqs, groups, wide),
         out_shape=(
-            jax.ShapeDtypeStruct((points, vectors, steps), f32),
+            jax.ShapeDtypeStruct((points * vectors, wide), f32),
             jax.ShapeDtypeStruct((8, LANES), f32),
         ),
         in_specs=[hbm, hbm, hbm, hbm, vmem],
@@ -723,7 +768,7 @@
             dma((CHUNKS, lines)), dma((CHUNKS, lines)),
             dma((CHUNKS, 2 * lines)), dma((CHUNKS, 2 * lines)),
             dma((CHUNKS,)), dma((CHUNKS,)),
-            dma((pieces,)), dma((pieces,)),
+            dma((BATCHES,)), dma((BATCHES,)),
             dma((1,)), dma((1,)),
             dma((n,)), dma((n,)),
         ],
@@ -731,7 +776,12 @@
             collective_id=0, has_side_effects=True, vmem_limit_bytes=60 * 1024 * 1024
         ),
     )(data, turned, jnp.asarray(forward), jnp.asarray(backward), jnp.asarray(maps))
-    return (jnp.transpose(fields, (1, 0, 2)), scale[0, :vectors])
+    return pl.pallas_call(
+        finish_kernel,
+        out_shape=(jax.ShapeDtypeStruct((vectors, points, steps), f32), jax.ShapeDtypeStruct((vectors,), f32)),
+        in_specs=[vmem, vmem],
+        out_specs=(vmem, vmem),
+    )(fields, scale)
 
 
 def solution(mesh):

time: 73.4 us -> 65.9 us (0.90)
  Pallas kernels: 69.6 us -> 65 us
  local copies, waits for them, and re-layouts: 2.84 us -> 0 us
    pallas_call x1, Pallas kernels: 69.6 us -> 63.3 us  [paired_body(): pl.pallas_call(functools.partial(kernel, n, lines, vectors, local, steps,...]
    pallas_call x0 -> x1, Pallas kernels: none -> 1.68 us  [paired_body(): pl.pallas_call(finish_kernel, out_shape=(jax.ShapeDtypeStruct((vectors, p...]
    unnamed x1 -> x0, local copies, waits for them, and re-layouts: 1.65 us -> none
    squeeze x1 -> x0, local copies, waits for them, and re-layouts: 1.2 us -> none  [paired_body(): return (jnp.transpose(fields, (1, 0, 2)), scale[0, :vectors])]
where the time goes in v2:
time: 65.9 us; the launch traced here: 65.6 us
  Pallas kernels  65 us (99%)
    pallas_call x1, Pallas kernels, paired_body(): pl.pallas_call(functools.partial(kernel, n, lines, vectors, local, steps,...  63.3 us
    pallas_call x1, Pallas kernels, paired_body(): pl.pallas_call(finish_kernel, out_shape=(jax.ShapeDtypeStruct((vectors, p...  1.68 us

profile of v2, /device:TPU:0, one launch (start us, length us, event | category | flops | bytes accessed | tf_op | source)
XLA Modules:
  0.0 65.6 jit_solution(11374204396062515092)
XLA Ops:
  0.6 63.3 %shard_map.68 = (f32[64,512]{1,0:T(8,128)}, f32[8,128]{1,0:T(8,128)}) custom-call(f32[16,16,420]{2,1,0:T(8,128)} %data_ref.1, f32[2,421,8,128]{3,2,1,0:T(8,128)} %bitcast.7, bf16[2,6,448,128]{3,2,1,0:T(8,128)(2,1)} %constant.6.clone.forward_ref, bf16[2,2,2,224,512]{4,3,2,1,0:T(8,128)(2,1)} %constant.7.clone.backward_ref, s32[8,512]{1,0:T(8,128)} %constant.8.clone.maps_ref), custom_call_target="tpu_custom_call" | custom-call | tf_op jit(solution)/shard_map/pallas_call | solution.py:738
  63.9 1.7 %shard_map.69 = (f32[16,4,420]{2,1,0:T(4,128)}, f32[16]{0:T(128)}) custom-call(f32[64,512]{1,0:T(8,128)} %get-tuple-element.4.field_ref, f32[8,128]{1,0:T(8,128)} %get-tuple-element.5.scale_ref), custom_call_target="tpu_custom_call" | custom-call | tf_op jit(solution)/shard_map/pallas_call | solution.py:779

commit v3 on v2

--- a/solution.py
+++ b/solution.py
@@ -208,6 +208,7 @@
     count = groups * GROUP
     pieces = groups // PIECE
     span = PIECE * 2 * GROUP
+    batch = groups // BATCHES
 
     barrier = pltpu.get_barrier_semaphore()
 
@@ -296,7 +297,7 @@
         return pltpu.make_async_remote_copy(
             src_ref=packed.at[1 - x, :, pl.ds(begin, size), target],
             dst_ref=kbuf.at[1 + rel, :, pl.ds(begin, size)],
-            send_sem=k_send.at[piece, target], recv_sem=k_recv.at[piece, 1 + rel],
+            send_sem=k_send.at[target], recv_sem=k_recv.at[piece // (pieces // BATCHES)],
             device_id=(other_chip, target), device_id_type=MESH,
         )
 
@@ -305,27 +306,26 @@
         return pltpu.make_async_remote_copy(
             src_ref=packed.at[x, :, pl.ds(begin, PIECE), other_core],
             dst_ref=kbuf.at[0, :, pl.ds(begin, PIECE)],
-            send_sem=k_send.at[piece, 2], recv_sem=k_recv.at[piece, 0],
+            send_sem=k_send.at[2], recv_sem=k_recv.at[piece // (pieces // BATCHES)],
             device_id=(me, other_core), device_id_type=MESH,
         )
 
-    def k_arrival(piece, slot, size):
-        begin = piece * PIECE
+    def all_of(ref, send_sem, recv_sem):
         return pltpu.make_async_remote_copy(
-            src_ref=packed.at[0, :, pl.ds(begin, size), 0],
-            dst_ref=kbuf.at[slot, :, pl.ds(begin, size)],
-            send_sem=k_send.at[piece, 2], recv_sem=k_recv.at[piece, slot],
+            src_ref=ref, dst_ref=ref, send_sem=send_sem, recv_sem=recv_sem,
             device_id=(me, other_core), device_id_type=MESH,
         )
 
-    def wait_piece(piece):
-        k_arrival(piece, 0, PIECE).wait_recv()
-        for target in range(2):
-
-            @pl.when(core == target)
-            def _():
-                for arrival in range(1, 3):
-                    k_arrival(piece, arrival, filled(piece, target)).wait_recv()
+    def wait_batch(turn):
+        begin = turn * batch
+        full = all_of(kbuf.at[:, :, pl.ds(begin, batch)], k_send.at[2], k_recv.at[turn])
+        missing = 0 if turn + 1 < BATCHES else 2 * (PIECE - filled(pieces - 1, 1))
+        if missing:
+            short = all_of(packed.at[0, 0, pl.ds(0, 3 * batch - missing)], k_send.at[2], k_recv.at[turn])
+            pl.when(core == 0)(full.wait_recv)
+            pl.when(core == 1)(short.wait_recv)
+        else:
+            full.wait_recv()
 
     def send_piece(piece):
         for target in range(2):
@@ -381,20 +381,33 @@
             device_id=target, device_id_type=MESH,
         )
 
+    def some(blocks, send_sem, recv_sem):
+        return all_of(gathered.at[0, pl.ds(0, blocks * local)], send_sem, recv_sem)
+
+    def many(blocks, send_sem, recv_sem):
+        whole = gathered.shape[1] // local
+        if blocks <= whole:
+            return some(blocks, send_sem, recv_sem)
+        assert blocks % CHUNKS == 0
+        return all_of(gathered.at[:, pl.ds(0, blocks // CHUNKS * local)], send_sem, recv_sem)
+
+    def line_index(source, target):
+        return jnp.where(source < target, source, source - 1)
+
     def line_copy(chunk, step, way):
         source = jnp.clip(z - way * step, 0, lines - 1)
         target = jnp.clip(z + way, 0, lines - 1)
-        index = step if way > 0 else lines + step
         return send(
-            block(chunk, source, y), (slot(target, y, x), core), z_send.at[chunk, index], z_recv.at[chunk, index]
+            block(chunk, source, y), (slot(target, y, x), core),
+            z_send.at[0], z_recv.at[chunk, jnp.clip(line_index(source, target), 0, lines - 2)],
         )
 
     def line_arrival(chunk, step, way):
         source = jnp.clip(z - way * (step + 1), 0, lines - 1)
         target = jnp.clip(z + way, 0, lines - 1)
-        index = step if way > 0 else lines + step
         return source, send(
-            block(chunk, source, y), (slot(target, y, x), core), z_send.at[chunk, index], z_recv.at[chunk, index]
+            block(chunk, source, y), (slot(target, y, x), core),
+            z_send.at[0], z_recv.at[chunk, jnp.clip(line_index(source, z), 0, lines - 2)],
         )
 
     def sends(step, way):
@@ -406,16 +419,14 @@
         return z >= step + 1 if way > 0 else z + step + 1 < lines
 
     def y_copy(chunk, line):
-        return send(block(chunk, line, y), (y_chip, core), y_send.at[chunk, line], y_recv.at[chunk, line])
-
-    def y_arrival(chunk, line):
-        return send(block(chunk, line, 1 - y), (y_chip, core), y_send.at[chunk, line], y_recv.at[chunk, line])
+        index = jnp.where(line == z, 0, 1)
+        return send(block(chunk, line, y), (y_chip, core), y_send.at[0], y_recv.at[chunk, index])
 
     def turn_copy(chunk):
-        return send(block(chunk, z, 1 - y), (slot(z_mate, y, x), core), w_send.at[chunk], w_recv.at[chunk])
+        return send(block(chunk, z, 1 - y), (slot(z_mate, y, x), core), w_send.at[0], w_recv.at[chunk])
 
     def turn_arrival(chunk):
-        return send(block(chunk, z_mate, 1 - y), (slot(z_mate, y, x), core), w_send.at[chunk], w_recv.at[chunk])
+        return send(block(chunk, z_mate, 1 - y), (slot(z_mate, y, x), core), w_send.at[0], w_recv.at[chunk])
 
     def turns(chunk):
         return chunk >= CHUNKS // 2
@@ -424,10 +435,9 @@
         return jnp.logical_not(jnp.logical_and(turns(chunk), line == z_mate))
 
     def core_copy(chunk, row, line):
-        index = row * lines + line
         return pltpu.make_async_remote_copy(
             src_ref=block(chunk, line, row), dst_ref=block(chunk, line, row, 1),
-            send_sem=c_send.at[chunk, index], recv_sem=c_recv.at[chunk, index],
+            send_sem=c_send.at[0], recv_sem=c_recv.at[chunk],
             device_id=(me, other_core), device_id_type=MESH,
         )
 
@@ -461,7 +471,7 @@
                 core_copy(chunk, y, source).start()
 
     def from_mate(chunk):
-        y_arrival(chunk, z).wait_recv()
+        some(1, y_send.at[0], y_recv.at[chunk, 0]).wait_recv()
         core_copy(chunk, 1 - y, z).start()
 
     def to_mate(chunk):
@@ -470,23 +480,20 @@
             turn_copy(chunk).start()
 
     def from_row(chunk):
+        @pl.when(turns(chunk))
+        def _():
+            some(lines - 2, y_send.at[0], y_recv.at[chunk, 1]).wait_recv()
+            turn_arrival(chunk).wait_recv()
+
+        @pl.when(jnp.logical_not(turns(chunk)))
+        def _():
+            some(lines - 1, y_send.at[0], y_recv.at[chunk, 1]).wait_recv()
+
         for step in range(1, lines):
-            line = lax.rem(z + step, lines)
-
-            @pl.when(by_row(chunk, line))
-            def _():
-                y_arrival(chunk, line).wait_recv()
-
-            @pl.when(jnp.logical_not(by_row(chunk, line)))
-            def _():
-                turn_arrival(chunk).wait_recv()
-
-            core_copy(chunk, 1 - y, line).start()
+            core_copy(chunk, 1 - y, lax.rem(z + step, lines)).start()
 
     def from_core(chunk):
-        for line in range(lines):
-            for row in range(2):
-                core_copy(chunk, row, line).wait_recv()
+        some(n // 2, c_send.at[0], c_recv.at[chunk]).wait_recv()
 
     lane_index = lax.broadcasted_iota(jnp.int32, (gathered.shape[1], LANES), 1)
 
@@ -547,7 +554,6 @@
     lane = lax.broadcasted_iota(jnp.int32, (2 * rows, LANES), 1)
     row = lax.broadcasted_iota(jnp.int32, (2 * rows, LANES), 0) // points % 2
     sign = jnp.where((lane % (2 * vectors) < vectors) == (row == 0), 1.0, -1.0)
-    batch = groups // BATCHES
     step_rows = batch * GROUP
     owner_lane = lax.broadcasted_iota(jnp.int32, (step_rows, LANES), 1) // (2 * vectors)
 
@@ -555,7 +561,7 @@
         place_rows = pl.ds(pl.multiple_of(turn * step_rows, GROUP), step_rows)
         return pltpu.make_async_remote_copy(
             src_ref=send_val.at[place_rows], dst_ref=recv_val.at[place_rows],
-            send_sem=v_send.at[turn], recv_sem=v_recv.at[turn],
+            send_sem=v_send.at[0], recv_sem=v_recv.at[0],
             device_id=(other_chip, core), device_id_type=MESH,
         )
 
@@ -565,8 +571,7 @@
 
             @pl.when(turn == which)
             def _():
-                for piece in range(which * batch // PIECE, (which + 1) * batch // PIECE):
-                    wait_piece(piece)
+                wait_batch(which)
 
         for step in range(batch):
             group = turn * batch + step
@@ -605,9 +610,7 @@
             target[pl.ds(pl.multiple_of(turn * step_rows, GROUP), step_rows), :] = merged
         value_copy(turn).start()
 
-    @pl.loop(0, BATCHES)
-    def _(turn):
-        value_copy(turn).wait_recv()
+    all_of(recv_val, v_send.at[0], v_recv.at[0]).wait_recv()
 
     own_val[:count, :] = own_val[:count, :] + recv_val[...]
     turned = own_val[...].T
@@ -644,14 +647,7 @@
 
     def square_copy(step):
         return pltpu.make_async_remote_copy(
-            src_ref=square, dst_ref=squares.at[me], send_sem=r_send.at[step], recv_sem=r_recv.at[step],
-            device_id=(lax.rem(me + step, n), core), device_id_type=MESH,
-        )
-
-    def square_arrival(step):
-        return pltpu.make_async_remote_copy(
-            src_ref=square, dst_ref=squares.at[lax.rem(me + n - step, n)],
-            send_sem=r_send.at[step], recv_sem=r_recv.at[step],
+            src_ref=square, dst_ref=squares.at[me], send_sem=r_send.at[0], recv_sem=r_recv.at[0],
             device_id=(lax.rem(me + step, n), core), device_id_type=MESH,
         )
 
@@ -659,39 +655,28 @@
     def _(step):
         square_copy(step).start()
 
-    @pl.loop(0, CHUNKS)
-    def _(chunk):
-        for step in range(lines - 1):
-            for way in (1, -1):
-
-                @pl.when(sends(step, way))
-                def _():
-                    line_copy(chunk, step, way).wait_send()
-
-        for line in range(lines):
-
-            @pl.when(by_row(chunk, line))
-            def _():
-                y_copy(chunk, line).wait_send()
-
-            for row in range(2):
-                core_copy(chunk, row, line).wait_send()
-
-        @pl.when(turns(chunk))
+    for line in range(lines):
+        ahead = line + 1 if line + 1 < lines else 0
+        back = lines - line if line > 0 else 0
+
+        @pl.when(z == line)
         def _():
-            turn_copy(chunk).wait_send()
-
-    for piece in range(pieces):
-        for target in range(2):
-            k_copy(piece, target).wait_send()
-        k_keep(piece).wait_send()
-    for turn in range(BATCHES):
-        value_copy(turn).wait_send()
+            many((ahead + back) * CHUNKS, z_send.at[0], z_recv.at[0, 0]).wait_send()
+
+    late = CHUNKS - CHUNKS // 2
+    all_of(
+        gathered.at[:, pl.ds(0, (lines * CHUNKS - late) * local // CHUNKS)], y_send.at[0], y_recv.at[0, 0]
+    ).wait_send()
+    some(late, w_send.at[0], w_recv.at[0]).wait_send()
+    all_of(gathered.at[:, pl.ds(0, gathered.shape[1] // 2)], c_send.at[0], c_recv.at[0]).wait_send()
+    for target in range(2):
+        all_of(packed.at[0, :, pl.ds(0, groups - PIECE + filled(pieces - 1, target)), target],
+               k_send.at[target], k_recv.at[0]).wait_send()
+    all_of(packed.at[0, :, :, 0], k_send.at[2], k_recv.at[0]).wait_send()
+    all_of(send_val, v_send.at[0], v_recv.at[0]).wait_send()
     field_copy.wait_send()
 
-    @pl.loop(1, n)
-    def _(step):
-        square_arrival(step).wait()
+    all_of(squares.at[pl.ds(0, n - 1)], r_send.at[0], r_recv.at[0]).wait()
 
     energy_all = squares[0]
     for device in range(1, n):
@@ -763,14 +748,14 @@
             pltpu.VMEM((n, 8, LANES), f32),
             dma((3,)),
             dma((pieces,)),
-            dma((pieces, 3)), dma((pieces, 3)),
-            dma((CHUNKS, 2 * lines)), dma((CHUNKS, 2 * lines)),
-            dma((CHUNKS, lines)), dma((CHUNKS, lines)),
-            dma((CHUNKS, 2 * lines)), dma((CHUNKS, 2 * lines)),
-            dma((CHUNKS,)), dma((CHUNKS,)),
-            dma((BATCHES,)), dma((BATCHES,)),
+            dma((3,)), dma((BATCHES,)),
+            dma((1,)), dma((CHUNKS, lines - 1)),
+            dma((1,)), dma((CHUNKS, 2)),
+            dma((1,)), dma((CHUNKS,)),
+            dma((1,)), dma((CHUNKS,)),
             dma((1,)), dma((1,)),
-            dma((n,)), dma((n,)),
+            dma((1,)), dma((1,)),
+            dma((1,)), dma((1,)),
         ],
         compiler_params=pltpu.CompilerParams(
             collective_id=0, has_side_effects=True, vmem_limit_bytes=60 * 1024 * 1024
@@ -793,7 +778,7 @@
     def body(data, spectra):
         vectors, local, _ = data.shape
         sensors, points = spectra.shape[1:3]
-        fits = local * n * 2 == 2 * sensors and sensors == 2 * LANES and vectors == 2 * CHUNKS
+        fits = local * n == sensors and local % 8 == 0 and sensors == 2 * LANES and vectors == 2 * CHUNKS
         fits = fits and points * 2 * vectors == LANES and folded_layout_fits(data.shape[2])
         return (paired_body if pair and fits else general_body)(data, spectra)
 

time: 65.9 us -> 62.9 us (0.954)
  Pallas kernels: 65 us -> 62 us
    pallas_call x1, Pallas kernels: 63.3 us -> 60.3 us  [paired_body(): pl.pallas_call(functools.partial(kernel, n, lines, vectors, local, steps,...]
where the time goes in v3:
time: 62.9 us; the launch traced here: 62.6 us
  Pallas kernels  62 us (99%)
  between operations  0.64 us (1%)
    pallas_call x1, Pallas kernels, paired_body(): pl.pallas_call(functools.partial(kernel, n, lines, vectors, local, steps,...  60.3 us
    pallas_call x1, Pallas kernels, paired_body(): pl.pallas_call(finish_kernel, out_shape=(jax.ShapeDtypeStruct((vectors, p...  1.68 us

profile of v3, /device:TPU:0, one launch (start us, length us, event | category | flops | bytes accessed | tf_op | source)
XLA Modules:
  0.0 62.6 jit_solution(7438357150117701921)
XLA Ops:
  0.6 60.3 %shard_map.68 = (f32[64,512]{1,0:T(8,128)}, f32[8,128]{1,0:T(8,128)}) custom-call(f32[16,16,420]{2,1,0:T(8,128)} %data_ref.1, f32[2,421,8,128]{3,2,1,0:T(8,128)} %bitcast.7, bf16[2,6,448,128]{3,2,1,0:T(8,128)(2,1)} %constant.6.clone.forward_ref, bf16[2,2,2,224,512]{4,3,2,1,0:T(8,128)(2,1)} %constant.7.clone.backward_ref, s32[8,512]{1,0:T(8,128)} %constant.8.clone.maps_ref), custom_call_target="tpu_custom_call" | custom-call | tf_op jit(solution)/shard_map/pallas_call | solution.py:723
  60.9 1.7 %shard_map.69 = (f32[16,4,420]{2,1,0:T(4,128)}, f32[16]{0:T(128)}) custom-call(f32[64,512]{1,0:T(8,128)} %get-tuple-element.4.field_ref, f32[8,128]{1,0:T(8,128)} %get-tuple-element.5.scale_ref), custom_call_target="tpu_custom_call" | custom-call | tf_op jit(solution)/shard_map/pallas_call | solution.py:764

commit v4 on v3

--- a/solution.py
+++ b/solution.py
@@ -105,7 +105,8 @@
     rest = half + 1 - LANES
     groups = -(-(steps + 1) // (2 * GROUP))
     fits = steps % 2 == 0 and 0 < rest < LANES and half - LANES - (LANES - rest) <= LANES - rest
-    return fits and groups % (PIECE * BATCHES) == 0
+    fits = fits and groups % (PIECE * BATCHES) == 0
+    return fits and BATCHES * batch_shares(groups // BATCHES * GROUP)[0][1] <= LANES
 
 
 def frequency_order(freqs, groups):
@@ -146,6 +147,11 @@
 def halves(values):
     high = values.astype(jnp.bfloat16)
     return high, (values - high.astype(np.float32)).astype(jnp.bfloat16)
+
+
+def batch_shares(batch):
+    first = -(-batch // (2 * GROUP)) * GROUP
+    return ((0, first), (first, batch - first))
 
 
 def paired_tables(steps, freqs, groups, rows_pad, wide):
@@ -175,10 +181,17 @@
             blocks.append(block.reshape(2 * rows_pad, LANES))
         forward.append(np.stack(blocks))
         weight = np.where((bins == 0) | (bins == steps), 0.5, 1.0)[:, None] / steps
-        inverse = np.zeros((2, 2, rows_pad, wide), jnp.bfloat16)
+        inverse = np.zeros((2, 2, 2, LANES, wide), jnp.bfloat16)
+        batch = groups // BATCHES * GROUP
         for position, table in enumerate((symmetric, other)):
             value = (table * weight).astype(np.float32)
-            inverse[0, position, :count, :steps], inverse[1, position, :count, :steps] = halves(value)
+            for turn in range(BATCHES):
+                for share, (begin, size) in enumerate(batch_shares(batch)):
+                    target = slice(turn * batch_shares(batch)[0][1], turn * batch_shares(batch)[0][1] + size)
+                    source = slice(turn * batch + begin, turn * batch + begin + size)
+                    parts = halves(value[source])
+                    for index in range(2):
+                        inverse[index, position, share, target, :steps] = parts[index]
         backward.append(inverse)
     return np.stack(forward), np.stack(backward)
 
@@ -236,19 +249,19 @@
 
     data_copy = pltpu.make_async_copy(data_ref, series, load_sem.at[0])
     forward_copy = pltpu.make_async_copy(forward_ref.at[core], table, load_sem.at[1])
-    backward_copy = pltpu.make_async_copy(
-        backward_ref.at[core], inverse.at[:, :, pl.ds(0, backward_ref.shape[3])], load_sem.at[2]
-    )
+    backward_copies = [
+        pltpu.make_async_copy(backward_ref.at[source], inverse.at[index], load_sem.at[2 + index])
+        for index, source in enumerate((core, other_core))
+    ]
     raw_copy(0).start()
     data_copy.start()
     for piece in range(1, pieces):
         raw_copy(piece).start()
     forward_copy.start()
-    backward_copy.start()
+    for backward_copy in backward_copies:
+        backward_copy.start()
 
     raw[:, freqs:] = jnp.zeros((2, raw.shape[1] - freqs) + tuple(raw.shape[2:]), jnp.float32)
-    pad = inverse.shape[2] - backward_ref.shape[3]
-    inverse[:, :, inverse.shape[2] - pad :, :] = jnp.zeros((2, 2, pad, wide), jnp.bfloat16)
     short = filled(pieces - 1, 1)
     if short < PIECE:
 
@@ -258,7 +271,6 @@
             for owner in range(1, 3):
                 kbuf[owner, :, begin:] = jnp.zeros((2, PIECE - short) + tuple(kbuf.shape[3:]), jnp.float32)
 
-    own_val[count:, :] = jnp.zeros((own_val.shape[0] - count, LANES), jnp.float32)
 
     strip = 64
 
@@ -352,7 +364,7 @@
     plain = (((1,), (0,)), ((), ()))
     folded = []
     for side in range(2):
-        values = jnp.concatenate([series[2 * chunk + side] for chunk in range(CHUNKS)], axis=0)
+        values = jnp.concatenate([series[side * CHUNKS + chunk] for chunk in range(CHUNKS)], axis=0)
         high = values.astype(jnp.bfloat16)
         left = values - high.astype(jnp.float32)
         middle = left.astype(jnp.bfloat16)
@@ -514,7 +526,7 @@
             left = jnp.concatenate([table[position], table[2 + which]], axis=1)
             result = split_product(left, count, right)
             for lane in range(2):
-                spectrum[lane, pl.ds(position * vectors + 2 * chunk + odd, count, stride=2 * vectors), :] = result[
+                spectrum[lane, pl.ds(odd * vectors + position * CHUNKS + chunk, count, stride=2 * vectors), :] = result[
                     :, lane * LANES : (lane + 1) * LANES
                 ]
 
@@ -526,7 +538,8 @@
         send_piece(piece)
 
     forward_copy.wait()
-    backward_copy.wait()
+    for backward_copy in backward_copies:
+        backward_copy.wait()
 
     def finish(chunk):
         from_core(chunk)
@@ -553,16 +566,31 @@
     own = row_freq == col_freq
     lane = lax.broadcasted_iota(jnp.int32, (2 * rows, LANES), 1)
     row = lax.broadcasted_iota(jnp.int32, (2 * rows, LANES), 0) // points % 2
-    sign = jnp.where((lane % (2 * vectors) < vectors) == (row == 0), 1.0, -1.0)
-    step_rows = batch * GROUP
-    owner_lane = lax.broadcasted_iota(jnp.int32, (step_rows, LANES), 1) // (2 * vectors)
-
-    def value_copy(turn):
-        place_rows = pl.ds(pl.multiple_of(turn * step_rows, GROUP), step_rows)
+    first_half = lane % vectors < vectors // 2
+    sign = jnp.where(first_half == (row == 0), 1.0, -1.0)
+    shares = batch_shares(batch * GROUP)
+    step_rows = shares[0][1]
+    lane_group = lax.broadcasted_iota(jnp.int32, (step_rows, LANES), 1) // vectors
+    known_rows = lax.broadcasted_iota(jnp.int32, (step_rows, LANES), 0) < shares[1][1]
+
+    def value_rows(turn):
+        return pl.ds(pl.multiple_of(turn * step_rows, GROUP), step_rows)
+
+    def value_copy(turn, target):
+        place_rows = value_rows(turn)
         return pltpu.make_async_remote_copy(
-            src_ref=send_val.at[place_rows], dst_ref=recv_val.at[place_rows],
+            src_ref=send_val.at[target, place_rows],
+            dst_ref=recv_val.at[jnp.where(core == target, 0, 2), place_rows],
             send_sem=v_send.at[0], recv_sem=v_recv.at[0],
-            device_id=(other_chip, core), device_id_type=MESH,
+            device_id=(other_chip, target), device_id_type=MESH,
+        )
+
+    def value_keep(turn):
+        place_rows = value_rows(turn)
+        return pltpu.make_async_remote_copy(
+            src_ref=send_val.at[2, place_rows], dst_ref=recv_val.at[1, place_rows],
+            send_sem=v_send.at[0], recv_sem=v_recv.at[0],
+            device_id=(me, other_core), device_id_type=MESH,
         )
 
     @pl.loop(0, BATCHES)
@@ -595,65 +623,88 @@
             while hop >= 2 * vectors:
                 found = found + pltpu.roll(found, hop, 1)
                 hop //= 2
-            value = found[: 2 * rows] + sign * pltpu.roll(found[2 * rows :], vectors, 1)
+            turned = found[2 * rows :]
+            turned = jnp.where(
+                first_half, pltpu.roll(turned, LANES - vectors // 2, 1), pltpu.roll(turned, vectors // 2, 1)
+            )
+            value = found[: 2 * rows] + sign * turned
             for owner in range(2):
                 product_s[owner, pl.ds(pl.multiple_of(group * rows, rows), rows), :] = value[
                     owner * rows : (owner + 1) * rows
                 ]
-        begin = turn * batch * rows
-        for owner, target in ((1, send_val), (0, own_val)):
-            merged = jnp.zeros((step_rows, LANES), jnp.float32)
-            for point in range(points):
-                merged = jnp.where(
-                    owner_lane == point, product_s[owner, pl.ds(begin + point, step_rows, stride=points), :], merged
-                )
-            target[pl.ds(pl.multiple_of(turn * step_rows, GROUP), step_rows), :] = merged
-        value_copy(turn).start()
-
-    all_of(recv_val, v_send.at[0], v_recv.at[0]).wait_recv()
-
-    own_val[:count, :] = own_val[:count, :] + recv_val[...]
-    turned = own_val[...].T
-    by_position = []
-    for position in range(2):
-        by_position.append(jnp.concatenate(
-            [turned[(2 * point + position) * vectors : (2 * point + position + 1) * vectors] for point in range(points)],
-            axis=0,
-        ))
-    left = split(jnp.concatenate(by_position, axis=1))
-    deep = 2 * inverse.shape[2]
-    partial[...] = product(left, (inverse[0].reshape(deep, wide), inverse[1].reshape(deep, wide)), plain)
+        for owner in (1, 0):
+            merged = [jnp.zeros((step_rows, LANES), jnp.float32)] * 2
+            for share in range(2):
+                for point in range(points):
+                    begin = (turn * batch * GROUP + shares[share][0]) * points + point
+                    value = product_s[owner, pl.ds(begin, step_rows, stride=points), :]
+                    if share == 1:
+                        value = jnp.where(known_rows, value, 0.0)
+                    shifted = pltpu.roll(value, vectors, 1)
+                    index = share * points + point
+                    for target in range(2):
+                        chosen = value if index % 2 == target else shifted
+                        merged[target] = jnp.where(lane_group == index, chosen, merged[target])
+            if owner == 1:
+                for target in range(2):
+                    send_val[target, value_rows(turn), :] = merged[target]
+                for target in range(2):
+                    value_copy(turn, target).start()
+            else:
+                send_val[2, value_rows(turn), :] = jnp.where(core == 0, merged[1], merged[0])
+                own_val[value_rows(turn), :] = jnp.where(core == 0, merged[0], merged[1])
+                value_keep(turn).start()
+
+    sent = BATCHES * step_rows
+    all_of(recv_val.at[:, pl.ds(0, sent)], v_send.at[0], v_recv.at[0]).wait_recv()
+
+    own_half = vectors // 2
+    blocks = []
+    for near in (own_val[:sent, :] + recv_val[0, :sent, :], recv_val[1, :sent, :] + recv_val[2, :sent, :]):
+        turned = jnp.concatenate([near, jnp.zeros((LANES - sent, LANES), jnp.float32)], axis=0).T
+        for position in range(2):
+            for share in range(2):
+                begins = [
+                    ((share * points + point) * 2 + position) * own_half for point in range(points)
+                ]
+                blocks.append(jnp.concatenate([turned[begin : begin + own_half] for begin in begins], axis=0))
+    left = split(jnp.concatenate(blocks, axis=1))
+    right = []
+    for index in range(2):
+        right.append(jnp.concatenate([inverse[near, index].reshape(4 * LANES, wide) for near in range(2)], axis=0))
+    total = product(left, right, plain)
+    partial[...] = total
 
     field_copy = pltpu.make_async_remote_copy(
         src_ref=partial, dst_ref=pair, send_sem=f_send.at[0], recv_sem=f_recv.at[0],
         device_id=(me, other_core), device_id_type=MESH,
     )
-    field_copy.start()
-    field_copy.wait_recv()
-
-    total = partial[...] + pair[...]
+
     energy = total * total
-    summed = energy[:vectors]
+    summed = energy[:own_half]
     for point in range(1, points):
-        summed = summed + energy[point * vectors : (point + 1) * vectors]
-    diagonal = lax.broadcasted_iota(jnp.int32, (vectors, LANES), 0) == lax.broadcasted_iota(
-        jnp.int32, (vectors, LANES), 1
-    )
+        summed = summed + energy[point * own_half : (point + 1) * own_half]
     column = jnp.sum(summed, axis=1, keepdims=True)
-    flat = jnp.sum(jnp.where(diagonal, column, 0.0), axis=0, keepdims=True)
-    flat = jnp.broadcast_to(flat, (8, LANES))
+    lane8 = lax.broadcasted_iota(jnp.int32, (own_half, LANES), 1)
+    row8 = lax.broadcasted_iota(jnp.int32, (own_half, LANES), 0)
+    flat = jnp.sum(jnp.where(lane8 == row8 + core * own_half, column, 0.0), axis=0, keepdims=True)
     square[...] = flat
-    squares[me] = flat
-
-    def square_copy(step):
+    mine = core * n + me
+    squares[mine] = flat
+
+    def square_copy(target, target_core):
         return pltpu.make_async_remote_copy(
-            src_ref=square, dst_ref=squares.at[me], send_sem=r_send.at[0], recv_sem=r_recv.at[0],
-            device_id=(lax.rem(me + step, n), core), device_id_type=MESH,
+            src_ref=square, dst_ref=squares.at[mine], send_sem=r_send.at[0], recv_sem=r_recv.at[0],
+            device_id=(target, target_core), device_id_type=MESH,
         )
 
     @pl.loop(1, n)
     def _(step):
-        square_copy(step).start()
+        square_copy(lax.rem(me + step, n), core).start()
+        square_copy(lax.rem(me + step, n), other_core).start()
+
+    square_copy(me, other_core).start()
+    field_copy.start()
 
     for line in range(lines):
         ahead = line + 1 if line + 1 < lines else 0
@@ -673,17 +724,20 @@
         all_of(packed.at[0, :, pl.ds(0, groups - PIECE + filled(pieces - 1, target)), target],
                k_send.at[target], k_recv.at[0]).wait_send()
     all_of(packed.at[0, :, :, 0], k_send.at[2], k_recv.at[0]).wait_send()
-    all_of(send_val, v_send.at[0], v_recv.at[0]).wait_send()
+    all_of(send_val.at[:, pl.ds(0, sent)], v_send.at[0], v_recv.at[0]).wait_send()
     field_copy.wait_send()
 
-    all_of(squares.at[pl.ds(0, n - 1)], r_send.at[0], r_recv.at[0]).wait()
+    field_copy.wait_recv()
+    tall = points * own_half
+    out_ref[pl.ds(pl.multiple_of(core * tall, tall), tall), :] = total
+    out_ref[pl.ds(pl.multiple_of(other_core * tall, tall), tall), :] = pair[...]
+    all_of(squares.at[pl.ds(0, 2 * n - 1)], r_send.at[0], r_recv.at[0]).wait()
 
     energy_all = squares[0]
-    for device in range(1, n):
+    for device in range(1, 2 * n):
         energy_all = energy_all + squares[device]
     scale = jnp.sqrt(energy_all / (points * n * steps) + 1e-06)
-    rms_ref[...] = scale
-    out_ref[...] = total
+    rms_ref[...] = jnp.broadcast_to(scale, rms_ref.shape)
 
 
 def finish_kernel(field_ref, scale_ref, out_ref, rms_ref):
@@ -695,8 +749,11 @@
     )
     spread = jnp.broadcast_to(scale, (vectors, LANES))
     divisor = jnp.sum(jnp.where(diagonal, spread, 0.0), axis=1, keepdims=True)
+    half = vectors // 2
     for point in range(points):
-        out_ref[:, point, :] = field_ref[point * vectors : (point + 1) * vectors, :steps] / divisor
+        near = field_ref[point * half : (point + 1) * half, :steps]
+        far = field_ref[(points + point) * half : (points + point + 1) * half, :steps]
+        out_ref[:, point, :] = jnp.concatenate([near, far], axis=0) / divisor
 
 
 def paired_body(data, spectra):
@@ -707,7 +764,6 @@
     groups = -(-freqs // (2 * GROUP))
     count = groups * GROUP
     rows_pad = -(-count // 16) * 16
-    deep = -(-count // LANES) * LANES
     pieces = groups // PIECE
     lines = n // 4
     forward, backward = paired_tables(steps, freqs, groups, rows_pad, wide)
@@ -723,8 +779,8 @@
     fields, scale = pl.pallas_call(
         functools.partial(kernel, n, lines, vectors, local, steps, points, freqs, groups, wide),
         out_shape=(
-            jax.ShapeDtypeStruct((points * vectors, wide), f32),
-            jax.ShapeDtypeStruct((8, LANES), f32),
+            pltpu.VMEM((points * vectors, wide), f32),
+            pltpu.VMEM((8, LANES), f32),
         ),
         in_specs=[hbm, hbm, hbm, hbm, vmem],
         out_specs=(vmem, vmem),
@@ -736,17 +792,17 @@
             pltpu.VMEM((3, 2, groups, GROUP // 2, 2 * points, LANES), f32),
             pltpu.VMEM((CHUNKS, sensors, 7 * LANES), f32),
             pltpu.VMEM((6, 2 * rows_pad, LANES), bf16),
-            pltpu.VMEM((2, 2, deep, wide), bf16),
+            pltpu.VMEM((2, 2, 2, 2, LANES, wide), bf16),
             pltpu.VMEM((2, count * 2 * vectors, LANES), f32),
-            pltpu.VMEM((2, count * points, LANES), f32),
-            pltpu.VMEM((deep, LANES), f32),
-            pltpu.VMEM((count, LANES), f32),
-            pltpu.VMEM((count, LANES), f32),
-            pltpu.VMEM((points * vectors, wide), f32),
-            pltpu.VMEM((points * vectors, wide), f32),
-            pltpu.VMEM((8, LANES), f32),
-            pltpu.VMEM((n, 8, LANES), f32),
-            dma((3,)),
+            pltpu.VMEM((2, (count + GROUP) * points, LANES), f32),
+            pltpu.VMEM((LANES, LANES), f32),
+            pltpu.VMEM((3, LANES, LANES), f32),
+            pltpu.VMEM((3, LANES, LANES), f32),
+            pltpu.VMEM((points * vectors // 2, wide), f32),
+            pltpu.VMEM((points * vectors // 2, wide), f32),
+            pltpu.VMEM((1, LANES), f32),
+            pltpu.VMEM((2 * n, 1, LANES), f32),
+            dma((4,)),
             dma((pieces,)),
             dma((3,)), dma((BATCHES,)),
             dma((1,)), dma((CHUNKS, lines - 1)),
@@ -766,7 +822,7 @@
         out_shape=(jax.ShapeDtypeStruct((vectors, points, steps), f32), jax.ShapeDtypeStruct((vectors,), f32)),
         in_specs=[vmem, vmem],
         out_specs=(vmem, vmem),
-    )(fields, scale)
+    )(pltpu.with_memory_space_constraint(fields, pltpu.VMEM), pltpu.with_memory_space_constraint(scale, pltpu.VMEM))
 
 
 def solution(mesh):

time: 62.9 us -> 61.2 us (0.973)
  Pallas kernels: 62 us -> 60.3 us
    pallas_call x1, Pallas kernels: 1.68 us -> 0.77 us  [paired_body(): pl.pallas_call(finish_kernel, out_shape=(jax.ShapeDtypeStruct((vectors, p...]
    pallas_call x1, Pallas kernels: 60.3 us -> 59.5 us  [paired_body(): pl.pallas_call(functools.partial(kernel, n, lines, vectors, local, steps,...]
where the time goes in v4:
time: 61.2 us; the launch traced here: 61 us
  Pallas kernels  60.3 us (99%)
  between operations  0.64 us (1%)
    pallas_call x1, Pallas kernels, paired_body(): pl.pallas_call(functools.partial(kernel, n, lines, vectors, local, steps,...  59.5 us

profile of v4, /device:TPU:0, one launch (start us, length us, event | category | flops | bytes accessed | tf_op | source)
XLA Modules:
  0.0 61.0 jit_solution(11796559287106264344)
XLA Ops:
  0.6 59.5 %shard_map.68 = (f32[64,512]{1,0:T(8,128)S(1)}, f32[8,128]{1,0:T(8,128)S(1)}) custom-call(f32[16,16,420]{2,1,0:T(8,128)} %data_ref.1, f32[2,421,8,128]{3,2,1,0:T(8,128)} %bitcast.7, bf16[2,6,448,128]{3,2,1,0:T(8,128)(2,1)} %constant.6.clone.forward_ref, bf16[2,2,2,2,128,512]{5,4,3,2,1,0:T(8,128)(2,1)} %constant.7.clone.backward_ref, ...), custom_call_target="tpu_custom_call" | custom-call | tf_op jit(solution)/shard_map/pallas_call | solution.py:779
  60.2 0.8 %shard_map.69 = (f32[16,4,420]{2,1,0:T(4,128)}, f32[16]{0:T(128)}) custom-call(f32[64,512]{1,0:T(8,128)S(1)} %get-tuple-element.4.field_ref, f32[8,128]{1,0:T(8,128)S(1)} %get-tuple-element.5.scale_ref), custom_call_target="tpu_custom_call" | custom-call | tf_op jit(solution)/shard_map/pallas_call | solution.py:820

commit v5 on v4

--- a/solution.py
+++ b/solution.py
@@ -253,24 +253,13 @@
         pltpu.make_async_copy(backward_ref.at[source], inverse.at[index], load_sem.at[2 + index])
         for index, source in enumerate((core, other_core))
     ]
+    data_copy.start()
     raw_copy(0).start()
-    data_copy.start()
     for piece in range(1, pieces):
         raw_copy(piece).start()
     forward_copy.start()
     for backward_copy in backward_copies:
         backward_copy.start()
-
-    raw[:, freqs:] = jnp.zeros((2, raw.shape[1] - freqs) + tuple(raw.shape[2:]), jnp.float32)
-    short = filled(pieces - 1, 1)
-    if short < PIECE:
-
-        @pl.when(core == 1)
-        def _():
-            begin = (pieces - 1) * PIECE + short
-            for owner in range(1, 3):
-                kbuf[owner, :, begin:] = jnp.zeros((2, PIECE - short) + tuple(kbuf.shape[3:]), jnp.float32)
-
 
     strip = 64
 
@@ -343,11 +332,6 @@
         for target in range(2):
             k_copy(piece, target).start()
         k_keep(piece).start()
-
-    raw_copy(0).wait()
-    sort_piece(0)
-    pl.semaphore_wait(barrier, 4 + jnp.minimum(z, 1) + jnp.minimum(lines - 1 - z, 1))
-    send_piece(0)
 
     def slot(line, row, column):
         return line * plane + row * 2 + column
@@ -530,9 +514,21 @@
                     :, lane * LANES : (lane + 1) * LANES
                 ]
 
+    pl.semaphore_wait(barrier, 4 + jnp.minimum(z, 1) + jnp.minimum(lines - 1 - z, 1))
     pl.loop(0, CHUNKS)(start_lines)
 
-    for piece in range(1, pieces):
+    raw[:, freqs:] = jnp.zeros((2, raw.shape[1] - freqs) + tuple(raw.shape[2:]), jnp.float32)
+    short = filled(pieces - 1, 1)
+    if short < PIECE:
+
+        @pl.when(core == 1)
+        def _():
+            begin = (pieces - 1) * PIECE + short
+            for owner in range(1, 3):
+                kbuf[owner, :, begin:] = jnp.zeros((2, PIECE - short) + tuple(kbuf.shape[3:]), jnp.float32)
+
+
+    for piece in range(pieces):
         raw_copy(piece).wait()
         sort_piece(piece)
         send_piece(piece)
@@ -547,11 +543,11 @@
 
     stages = [
         (functools.partial(from_lines, step=0), 0), (from_mate, 0),
-        (functools.partial(from_lines, step=1), 1), (functools.partial(from_lines, step=2), 2),
-        (to_mate, 4), (from_row, 6), (finish, 7),
+        (functools.partial(from_lines, step=1), 1), (functools.partial(from_lines, step=2), 2), (to_mate, 3),
+        (from_row, 5), (finish, 6),
     ]
 
-    @pl.loop(0, CHUNKS + 7)
+    @pl.loop(0, CHUNKS + stages[-1][1])
     def _(turn):
         for stage, age in stages:
             chunk = turn - age

time: 61.2 us -> 60.2 us (0.984)
  Pallas kernels: 60.3 us -> 59.3 us
    pallas_call x1, Pallas kernels: 59.5 us -> 58.5 us  [paired_body(): pl.pallas_call(functools.partial(kernel, n, lines, vectors, local, steps,...]
where the time goes in v5:
time: 60.2 us; the launch traced here: 59.9 us
  Pallas kernels  59.3 us (99%)
  between operations  0.64 us (1%)
    pallas_call x1, Pallas kernels, paired_body(): pl.pallas_call(functools.partial(kernel, n, lines, vectors, local, steps,...  58.5 us

profile of v5, /device:TPU:0, one launch (start us, length us, event | category | flops | bytes accessed | tf_op | source)
XLA Modules:
  0.0 59.9 jit_solution(5315584411069112838)
XLA Ops:
  0.6 58.5 %shard_map.68 = (f32[64,512]{1,0:T(8,128)S(1)}, f32[8,128]{1,0:T(8,128)S(1)}) custom-call(f32[16,16,420]{2,1,0:T(8,128)} %data_ref.1, f32[2,421,8,128]{3,2,1,0:T(8,128)} %bitcast.7, bf16[2,6,448,128]{3,2,1,0:T(8,128)(2,1)} %constant.6.clone.forward_ref, bf16[2,2,2,2,128,512]{5,4,3,2,1,0:T(8,128)(2,1)} %constant.7.clone.backward_ref, ...), custom_call_target="tpu_custom_call" | custom-call | tf_op jit(solution)/shard_map/pallas_call | solution.py:775
  59.2 0.8 %shard_map.69 = (f32[16,4,420]{2,1,0:T(4,128)}, f32[16]{0:T(128)}) custom-call(f32[64,512]{1,0:T(8,128)S(1)} %get-tuple-element.4.field_ref, f32[8,128]{1,0:T(8,128)S(1)} %get-tuple-element.5.scale_ref), custom_call_target="tpu_custom_call" | custom-call | tf_op jit(solution)/shard_map/pallas_call | solution.py:816

commit v6 on v5

--- a/solution.py
+++ b/solution.py
@@ -15,6 +15,7 @@
 CHUNKS = 8
 PIECE = 3
 BATCHES = 3
+PAD_ROWS = 4
 
 
 def spectral_tables(steps):
@@ -221,6 +222,7 @@
     count = groups * GROUP
     pieces = groups // PIECE
     span = PIECE * 2 * GROUP
+    pitch = 2 * vectors + PAD_ROWS
     batch = groups // BATCHES
 
     barrier = pltpu.get_barrier_semaphore()
@@ -510,7 +512,7 @@
             left = jnp.concatenate([table[position], table[2 + which]], axis=1)
             result = split_product(left, count, right)
             for lane in range(2):
-                spectrum[lane, pl.ds(odd * vectors + position * CHUNKS + chunk, count, stride=2 * vectors), :] = result[
+                spectrum[lane, pl.ds(odd * vectors + position * CHUNKS + chunk, count, stride=pitch), :] = result[
                     :, lane * LANES : (lane + 1) * LANES
                 ]
 
@@ -543,8 +545,8 @@
 
     stages = [
         (functools.partial(from_lines, step=0), 0), (from_mate, 0),
-        (functools.partial(from_lines, step=1), 1), (functools.partial(from_lines, step=2), 2), (to_mate, 3),
-        (from_row, 5), (finish, 6),
+        (functools.partial(from_lines, step=1), 2), (functools.partial(from_lines, step=2), 3), (to_mate, 4),
+        (from_row, 6), (finish, 7),
     ]
 
     @pl.loop(0, CHUNKS + stages[-1][1])
@@ -599,10 +601,12 @@
 
         for step in range(batch):
             group = turn * batch + step
-            begin = pl.multiple_of(group * columns, columns)
-            right = split(
-                jnp.concatenate([spectrum[0, pl.ds(begin, columns), :], spectrum[1, pl.ds(begin, columns), :]], axis=1)
-            )
+            begin = pl.multiple_of(group * GROUP * pitch, GROUP)
+            sides = []
+            for side in range(2):
+                pieces_of = [spectrum[side, pl.ds(begin + step_f * pitch, 2 * vectors), :] for step_f in range(GROUP)]
+                sides.append(jnp.concatenate(pieces_of, axis=0))
+            right = split(jnp.concatenate(sides, axis=1))
             parts = []
             for part in range(2):
                 for near, far in (
@@ -789,7 +793,7 @@
             pltpu.VMEM((CHUNKS, sensors, 7 * LANES), f32),
             pltpu.VMEM((6, 2 * rows_pad, LANES), bf16),
             pltpu.VMEM((2, 2, 2, 2, LANES, wide), bf16),
-            pltpu.VMEM((2, count * 2 * vectors, LANES), f32),
+            pltpu.VMEM((2, count * (2 * vectors + PAD_ROWS), LANES), f32),
             pltpu.VMEM((2, (count + GROUP) * points, LANES), f32),
             pltpu.VMEM((LANES, LANES), f32),
             pltpu.VMEM((3, LANES, LANES), f32),

time: 60.2 us -> 58.5 us (0.972)
  Pallas kernels: 59.3 us -> 57.6 us
    pallas_call x1, Pallas kernels: 58.5 us -> 56.8 us  [paired_body(): pl.pallas_call(functools.partial(kernel, n, lines, vectors, local, steps,...]
where the time goes in v6:
time: 58.5 us; the launch traced here: 58.2 us
  Pallas kernels  57.6 us (98%)
  between operations  0.64 us (1%)
    pallas_call x1, Pallas kernels, paired_body(): pl.pallas_call(functools.partial(kernel, n, lines, vectors, local, steps,...  56.8 us

profile of v6, /device:TPU:0, one launch (start us, length us, event | category | flops | bytes accessed | tf_op | source)
XLA Modules:
  0.0 58.2 jit_solution(8099063960023903845)
XLA Ops:
  0.6 56.8 %shard_map.68 = (f32[64,512]{1,0:T(8,128)S(1)}, f32[8,128]{1,0:T(8,128)S(1)}) custom-call(f32[16,16,420]{2,1,0:T(8,128)} %data_ref.1, f32[2,421,8,128]{3,2,1,0:T(8,128)} %bitcast.7, bf16[2,6,448,128]{3,2,1,0:T(8,128)(2,1)} %constant.6.clone.forward_ref, bf16[2,2,2,2,128,512]{5,4,3,2,1,0:T(8,128)(2,1)} %constant.7.clone.backward_ref, ...), custom_call_target="tpu_custom_call" | custom-call | tf_op jit(solution)/shard_map/pallas_call | solution.py:779
  57.5 0.8 %shard_map.69 = (f32[16,4,420]{2,1,0:T(4,128)}, f32[16]{0:T(128)}) custom-call(f32[64,512]{1,0:T(8,128)S(1)} %get-tuple-element.4.field_ref, f32[8,128]{1,0:T(8,128)S(1)} %get-tuple-element.5.scale_ref), custom_call_target="tpu_custom_call" | custom-call | tf_op jit(solution)/shard_map/pallas_call | solution.py:820

commit v7 on v6

--- a/solution.py
+++ b/solution.py
@@ -16,6 +16,7 @@
 PIECE = 3
 BATCHES = 3
 PAD_ROWS = 4
+NARROW = 2
 
 
 def spectral_tables(steps):
@@ -105,7 +106,7 @@
     half = steps // 2
     rest = half + 1 - LANES
     groups = -(-(steps + 1) // (2 * GROUP))
-    fits = steps % 2 == 0 and 0 < rest < LANES and half - LANES - (LANES - rest) <= LANES - rest
+    fits = rest - 1 <= 2 * (LANES - (rest - 1)) and steps % 2 == 0 and 0 < rest < LANES and half - LANES - (LANES - rest) <= LANES - rest
     fits = fits and groups % (PIECE * BATCHES) == 0
     return fits and BATCHES * batch_shares(groups // BATCHES * GROUP)[0][1] <= LANES
 
@@ -344,7 +345,8 @@
 
     def block(chunk, line, row, rel=0):
         position = rel * (n // 2) + place(line, row)
-        return gathered.at[chunk, pl.ds(pl.multiple_of(position * local, local), local), :]
+        row_range = pl.ds(pl.multiple_of(position * local, local), local)
+        return gathered.at[chunk, row_range, pl.ds(0, wide_now[0] * LANES)]
 
     data_copy.wait()
     plain = (((1,), (0,)), ((), ()))
@@ -362,16 +364,35 @@
         size = CHUNKS * local
         folded.append(result[:size] + (result[size : 2 * size] + result[2 * size :]))
     own_row = pl.ds(pl.multiple_of(place(z, y) * local, local), local)
+    lane_index = lax.broadcasted_iota(jnp.int32, (gathered.shape[1], LANES), 1)
+    lane_small = lax.broadcasted_iota(jnp.int32, (local, LANES), 1)
+    spare = LANES - (rest - 1)
+
+    def folded_block(side, chunk, index):
+        return folded[side][chunk * local : (chunk + 1) * local, index * LANES : (index + 1) * LANES]
+
     for chunk in range(CHUNKS):
-        even = folded[0][chunk * local : (chunk + 1) * local]
-        odd = folded[1][chunk * local : (chunk + 1) * local]
-        gathered[chunk, own_row, 0 : 2 * LANES] = even[:, : 2 * LANES]
-        gathered[chunk, own_row, 2 * LANES : 4 * LANES] = odd[:, : 2 * LANES]
-        gathered[chunk, own_row, 4 * LANES : 5 * LANES] = (
-            even[:, 2 * LANES : 3 * LANES] + odd[:, 2 * LANES : 3 * LANES]
-        )
-        gathered[chunk, own_row, 5 * LANES : 6 * LANES] = even[:, 3 * LANES :]
-        gathered[chunk, own_row, 6 * LANES :] = odd[:, 3 * LANES :]
+        for index in range(2):
+            gathered[chunk, own_row, index * LANES : (index + 1) * LANES] = folded_block(0, chunk, index)
+            gathered[chunk, own_row, (2 + index) * LANES : (3 + index) * LANES] = folded_block(1, chunk, index)
+        gathered[chunk, own_row, 4 * LANES : 5 * LANES] = folded_block(0, chunk, 2) + folded_block(1, chunk, 2)
+        gathered[chunk, own_row, 5 * LANES : 6 * LANES] = folded_block(1, chunk, 3)
+        if chunk < CHUNKS - NARROW:
+            last = folded_block(0, chunk, 3)
+            if chunk < 2 * NARROW:
+                guest = folded_block(0, CHUNKS - NARROW + chunk // 2, 3)
+                shift = rest - 1 - chunk % 2 * spare
+                last = jnp.where(lane_small >= rest - 1, pltpu.roll(guest, shift, 1), last)
+            gathered[chunk, own_row, 6 * LANES :] = last
+
+    def unpack(chunk):
+        source = 2 * (chunk - (CHUNKS - NARROW))
+        begin = 6 * LANES
+        near = pltpu.roll(gathered[source, :, begin:], spare, 1)
+        far = pltpu.roll(gathered[source + 1, :, begin:], LANES - (rest - 1 - spare), 1)
+        gathered[chunk, :, begin:] = jnp.where(lane_index < spare, near, far)
+
+    wide_now = [7]
 
     def send(source, target, send_sem, recv_sem):
         return pltpu.make_async_remote_copy(
@@ -380,14 +401,13 @@
         )
 
     def some(blocks, send_sem, recv_sem):
-        return all_of(gathered.at[0, pl.ds(0, blocks * local)], send_sem, recv_sem)
-
-    def many(blocks, send_sem, recv_sem):
-        whole = gathered.shape[1] // local
-        if blocks <= whole:
-            return some(blocks, send_sem, recv_sem)
-        assert blocks % CHUNKS == 0
-        return all_of(gathered.at[:, pl.ds(0, blocks // CHUNKS * local)], send_sem, recv_sem)
+        return all_of(gathered.at[0, pl.ds(0, blocks * local), pl.ds(0, wide_now[0] * LANES)], send_sem, recv_sem)
+
+    def tiles(number, send_sem, recv_sem):
+        if number <= raw.shape[1]:
+            return all_of(raw.at[0, pl.ds(0, number)], send_sem, recv_sem)
+        assert number % 2 == 0
+        return all_of(raw.at[:, pl.ds(0, number // 2)], send_sem, recv_sem)
 
     def line_index(source, target):
         return jnp.where(source < target, source, source - 1)
@@ -493,7 +513,6 @@
     def from_core(chunk):
         some(n // 2, c_send.at[0], c_recv.at[chunk]).wait_recv()
 
-    lane_index = lax.broadcasted_iota(jnp.int32, (gathered.shape[1], LANES), 1)
 
     def transform(chunk):
         def lanes(index):
@@ -503,11 +522,11 @@
             odd = which // 2
             position = which % 2
             if which < 2:
-                tail = lanes(4 + which)
+                tail = lanes(4 + 2 * which)
             elif which == 2:
-                tail = lanes(6)
+                tail = lanes(5)
             else:
-                tail = jnp.where(lane_index >= rest, lanes(4), lanes(6))
+                tail = jnp.where(lane_index >= rest, lanes(4), lanes(5))
             right = split(jnp.concatenate([lanes(which), tail], axis=1))
             left = jnp.concatenate([table[position], table[2 + which]], axis=1)
             result = split_product(left, count, right)
@@ -517,7 +536,15 @@
                 ]
 
     pl.semaphore_wait(barrier, 4 + jnp.minimum(z, 1) + jnp.minimum(lines - 1 - z, 1))
-    pl.loop(0, CHUNKS)(start_lines)
+    def at_width(blocks, action):
+        def run(chunk):
+            wide_now[0] = blocks
+            action(chunk)
+
+        return run
+
+    pl.loop(0, CHUNKS - NARROW)(at_width(7, start_lines))
+    pl.loop(CHUNKS - NARROW, CHUNKS)(at_width(6, start_lines))
 
     raw[:, freqs:] = jnp.zeros((2, raw.shape[1] - freqs) + tuple(raw.shape[2:]), jnp.float32)
     short = filled(pieces - 1, 1)
@@ -540,23 +567,30 @@
         backward_copy.wait()
 
     def finish(chunk):
-        from_core(chunk)
+        @pl.when(chunk >= CHUNKS - NARROW)
+        def _():
+            unpack(chunk)
+
         transform(chunk)
 
     stages = [
         (functools.partial(from_lines, step=0), 0), (from_mate, 0),
         (functools.partial(from_lines, step=1), 2), (functools.partial(from_lines, step=2), 3), (to_mate, 4),
-        (from_row, 6), (finish, 7),
+        (from_row, 6), (from_core, 7),
     ]
-
-    @pl.loop(0, CHUNKS + stages[-1][1])
+    last_age = stages[-1][1]
+
+    @pl.loop(0, CHUNKS + last_age)
     def _(turn):
         for stage, age in stages:
             chunk = turn - age
-
-            @pl.when(jnp.logical_and(chunk >= 0, chunk < CHUNKS))
-            def _():
-                stage(chunk)
+            for blocks, begin, end in ((7, 0, CHUNKS - NARROW), (6, CHUNKS - NARROW, CHUNKS)):
+
+                @pl.when(jnp.logical_and(chunk >= begin, chunk < end))
+                def _():
+                    at_width(blocks, stage)(chunk)
+
+        pl.when(turn >= last_age)(lambda: finish(turn - last_age))
 
     columns = GROUP * 2 * vectors
     row_freq = lax.broadcasted_iota(jnp.int32, (4 * rows, columns), 0) // points % GROUP
@@ -706,20 +740,20 @@
     square_copy(me, other_core).start()
     field_copy.start()
 
+    block_tiles = local // 8
+    every = sum(7 if chunk < CHUNKS - NARROW else 6 for chunk in range(CHUNKS)) * block_tiles
+    late = sum(7 if chunk < CHUNKS - NARROW else 6 for chunk in range(CHUNKS // 2, CHUNKS)) * block_tiles
     for line in range(lines):
         ahead = line + 1 if line + 1 < lines else 0
         back = lines - line if line > 0 else 0
 
         @pl.when(z == line)
         def _():
-            many((ahead + back) * CHUNKS, z_send.at[0], z_recv.at[0, 0]).wait_send()
-
-    late = CHUNKS - CHUNKS // 2
-    all_of(
-        gathered.at[:, pl.ds(0, (lines * CHUNKS - late) * local // CHUNKS)], y_send.at[0], y_recv.at[0, 0]
-    ).wait_send()
-    some(late, w_send.at[0], w_recv.at[0]).wait_send()
-    all_of(gathered.at[:, pl.ds(0, gathered.shape[1] // 2)], c_send.at[0], c_recv.at[0]).wait_send()
+            tiles((ahead + back) * every, z_send.at[0], z_recv.at[0, 0]).wait_send()
+
+    tiles(lines * every - late, y_send.at[0], y_recv.at[0, 0]).wait_send()
+    tiles(late, w_send.at[0], w_recv.at[0]).wait_send()
+    tiles(n // 2 * every, c_send.at[0], c_recv.at[0]).wait_send()
     for target in range(2):
         all_of(packed.at[0, :, pl.ds(0, groups - PIECE + filled(pieces - 1, target)), target],
                k_send.at[target], k_recv.at[0]).wait_send()

time: 58.5 us -> 57.8 us (0.988)
  Pallas kernels: 57.6 us -> 56.9 us
    pallas_call x1, Pallas kernels: 56.8 us -> 56.2 us  [paired_body(): pl.pallas_call(functools.partial(kernel, n, lines, vectors, local, steps,...]
where the time goes in v7:
time: 57.8 us; the launch traced here: 57.6 us
  Pallas kernels  56.9 us (98%)
  between operations  0.64 us (1%)
    pallas_call x1, Pallas kernels, paired_body(): pl.pallas_call(functools.partial(kernel, n, lines, vectors, local, steps,...  56.2 us

profile of v7, /device:TPU:0, one launch (start us, length us, event | category | flops | bytes accessed | tf_op | source)
XLA Modules:
  0.0 57.6 jit_solution(15481567143126897287)
XLA Ops:
  0.6 56.2 %shard_map.68 = (f32[64,512]{1,0:T(8,128)S(1)}, f32[8,128]{1,0:T(8,128)S(1)}) custom-call(f32[16,16,420]{2,1,0:T(8,128)} %data_ref.1, f32[2,421,8,128]{3,2,1,0:T(8,128)} %bitcast.7, bf16[2,6,448,128]{3,2,1,0:T(8,128)(2,1)} %constant.6.clone.forward_ref, bf16[2,2,2,2,128,512]{5,4,3,2,1,0:T(8,128)(2,1)} %constant.7.clone.backward_ref, ...), custom_call_target="tpu_custom_call" | custom-call | tf_op jit(solution)/shard_map/pallas_call | solution.py:813
  56.8 0.8 %shard_map.69 = (f32[16,4,420]{2,1,0:T(4,128)}, f32[16]{0:T(128)}) custom-call(f32[64,512]{1,0:T(8,128)S(1)} %get-tuple-element.4.field_ref, f32[8,128]{1,0:T(8,128)S(1)} %get-tuple-element.5.scale_ref), custom_call_target="tpu_custom_call" | custom-call | tf_op jit(solution)/shard_map/pallas_call | solution.py:854

commit v8 on v7

--- a/solution.py
+++ b/solution.py
@@ -574,7 +574,7 @@
         transform(chunk)
 
     stages = [
-        (functools.partial(from_lines, step=0), 0), (from_mate, 0),
+        (functools.partial(from_lines, step=0), 0), (from_mate, 2),
         (functools.partial(from_lines, step=1), 2), (functools.partial(from_lines, step=2), 3), (to_mate, 4),
         (from_row, 6), (from_core, 7),
     ]
@@ -734,8 +734,9 @@
 
     @pl.loop(1, n)
     def _(step):
-        square_copy(lax.rem(me + step, n), core).start()
-        square_copy(lax.rem(me + step, n), other_core).start()
+        away = jnp.where(z < lines // 2, n - step, step)
+        square_copy(lax.rem(me + away, n), core).start()
+        square_copy(lax.rem(me + away, n), other_core).start()
 
     square_copy(me, other_core).start()
     field_copy.start()

time: 57.8 us -> 57.8 us (level)
  no operation moved by 1% of the time
where the time goes in v8:
time: 57.8 us; the launch traced here: 57.5 us
  Pallas kernels  56.9 us (98%)
  between operations  0.64 us (1%)
    pallas_call x1, Pallas kernels, paired_body(): pl.pallas_call(functools.partial(kernel, n, lines, vectors, local, steps,...  56.1 us

profile of v8, /device:TPU:0, one launch (start us, length us, event | category | flops | bytes accessed | tf_op | source)
XLA Modules:
  0.0 57.5 jit_solution(13851170544406386863)
XLA Ops:
  0.6 56.1 %shard_map.68 = (f32[64,512]{1,0:T(8,128)S(1)}, f32[8,128]{1,0:T(8,128)S(1)}) custom-call(f32[16,16,420]{2,1,0:T(8,128)} %data_ref.1, f32[2,421,8,128]{3,2,1,0:T(8,128)} %bitcast.7, bf16[2,6,448,128]{3,2,1,0:T(8,128)(2,1)} %constant.6.clone.forward_ref, bf16[2,2,2,2,128,512]{5,4,3,2,1,0:T(8,128)(2,1)} %constant.7.clone.backward_ref, ...), custom_call_target="tpu_custom_call" | custom-call | tf_op jit(solution)/shard_map/pallas_call | solution.py:814
  56.8 0.8 %shard_map.69 = (f32[16,4,420]{2,1,0:T(4,128)}, f32[16]{0:T(128)}) custom-call(f32[64,512]{1,0:T(8,128)S(1)} %get-tuple-element.4.field_ref, f32[8,128]{1,0:T(8,128)S(1)} %get-tuple-element.5.scale_ref), custom_call_target="tpu_custom_call" | custom-call | tf_op jit(solution)/shard_map/pallas_call | solution.py:855
